TPU v7x, 32 devices: a whole 2x2x4 slice. The times are simulated.
32 devices in a mesh: gx: 4 (over y, x), gy: 8 (over z, core).
Axes of the slice: x: 2, y: 2, z: 4, core: 2. Of those that a mesh axis runs over, the one named last changes fastest.
Arguments:
- u_wind: float32 [60, 256, 1024], P(None, 'gx', 'gy'), may hold values from -6 to 6
- v_wind: float32 [60, 256, 1024], P(None, 'gx', 'gy'), may hold values from -6 to 6
- w_wind: float32 [60, 256, 1024], P(None, 'gx', 'gy'), may hold values from -3 to 3
- pressure: float32 [60, 256, 1024], P(None, 'gx', 'gy'), may hold values from -6 to 6
- vert_coef: float32 [256, 1024], P('gx', 'gy'), may hold values from 0.2 to 5
- we_slab: float32 [2, 3, 60, 5, 1024], P(None, None, None, None, ('gy', 'gx')), may hold values from -8 to 8
- sn_slab: float32 [2, 3, 60, 5, 256], P(None, None, None, None, ('gx', 'gy')), may hold values from -8 to 8
- relax_width: int32 [256, 1024], P('gx', 'gy'), may hold values from 2 to 5
Outputs:
- u_out: float32 [60, 256, 1024], P(None, 'gx', 'gy')
- v_out: float32 [60, 256, 1024], P(None, 'gx', 'gy')
- w_out: float32 [60, 256, 1024], P(None, 'gx', 'gy')
- p_out: float32 [60, 256, 1024], P(None, 'gx', 'gy')
All inputs are finite; a program needn't handle non-finite values.
Results may differ from a plain program's by a relative error of at most 0.0001.
Values sent between devices are 32-bit elements; how exact they have to be, the bound alone decides.
No kernel may reach another device: no remote copies, remote signals or barrier semaphores. Data moves between devices by JAX's collectives and lax.ppermute only.
A program may use at most 192 MiB of HBM per device.

v0:
```python
import functools
import jax
import jax.numpy as jnp
from jax import lax
from jax.experimental import pallas as pl
from jax.experimental.pallas import tpu as pltpu
from jax.sharding import PartitionSpec as P

SUBSTEPS = 6
ACCEL = 0.3
SPREAD = 0.3
BUOYANCY = 0.5
DEEP = 6
GROUP = 2 * DEEP
ZC = 20
SUBL = 8
LANES = 128
F32 = jnp.float32


def lane_ids():
    return lax.broadcasted_iota(jnp.int32, (SUBL, LANES), 1)


def sub_ids():
    return lax.broadcasted_iota(jnp.int32, (SUBL, LANES), 0)


def lroll(x, shift):
    if isinstance(shift, int):
        shift = shift % LANES
        if shift == 0:
            return x
    return pltpu.roll(x, shift, 1)


def sroll(x, shift):
    return pltpu.roll(x, shift % SUBL, 0)


def pack_slabs(we, sn, west, east, south, north):
    band, m = we.shape[3], we.shape[4]
    xs = sn.shape[3]
    west[...] = jnp.zeros_like(west)
    east[...] = jnp.zeros_like(east)
    south[...] = jnp.zeros_like(south)
    north[...] = jnp.zeros_like(north)
    for f in range(3):
        for z in range(ZC):
            g, c = divmod(z, 4)
            west[0, f, g, 0:band, m * c : m * (c + 1)] = we[0, f, z]
            east[0, f, g, 0:band, m * c : m * (c + 1)] = we[1, f, z]
            t, c = divmod(z, 10)
            lo = GROUP * c
            s_val = sn[0, f, z]
            n_val = sn[1, f, z]
            for rep in range(SUBL // xs):
                rows = slice(xs * rep, xs * (rep + 1))
                south[0, f, t, rows, lo : lo + band] = s_val
                for d in range(band):
                    at = lo + band - 1 - d
                    north[0, f, t, rows, at : at + 1] = n_val[:, d : d + 1]


def blend_pack(n_gx, n_gy, m, xs, band, *refs):
    u, v, p, w, r, rate = refs[:6]
    refs = refs[6:]
    we_own = refs[:2]
    sn_own = refs[2:4]
    we_in = refs[4 : 4 + n_gx - 1]
    sn_in = refs[3 + n_gx : 3 + n_gx + n_gy - 1]
    ub, vb, pb, xa, xb, q, c_out = refs[2 + n_gx + n_gy :]
    gx = lax.axis_index("gx")
    gy = lax.axis_index("gy")
    size_x = u.shape[1]
    blocks = size_x // SUBL
    outs = (ub, vb, pb)
    for src, dst in zip((u, v, p), outs):
        dst[...] = src[...]
    lane = lane_ids()
    sub = sub_ids()

    def band_rows(pieces, f, z):
        g, c = z // 4, z % 4
        val = jnp.zeros((SUBL, LANES), F32)
        for s, piece in enumerate(pieces):
            moved = pltpu.roll(piece[0, f, g], jnp.mod(m * s - m * c, LANES), 1)
            val = jnp.where((lane >= m * s) & (lane < m * (s + 1)), moved, val)
        return val

    @pl.when(gx == 0)
    def _():
        pieces = [we_own[0]] + [we_in[s - 1] for s in range(1, n_gx)]
        rt = rate[0:SUBL, :].astype(F32)
        wt = jnp.maximum(rt - sub.astype(F32), 0.0) / rt

        def body(z, carry):
            for f in range(3):
                val = band_rows(pieces, f, z)
                old = outs[f][z, 0:SUBL, :]
                outs[f][z, 0:SUBL, :] = old + wt * (val - old)
            return carry

        lax.fori_loop(0, ZC, body, 0)

    @pl.when(gx == n_gx - 1)
    def _():
        pieces = [we_in[n_gx - 2 - s] for s in range(n_gx - 1)] + [we_own[1]]
        rt = rate[size_x - SUBL : size_x, :].astype(F32)
        wt = jnp.maximum(rt - (SUBL - 1 - sub).astype(F32), 0.0) / rt

        def body(z, carry):
            for f in range(3):
                val = band_rows(pieces, f, z)
                turned = sroll(val, 1)
                turned = jnp.where(sub % 4 == 1, sroll(val, 3), turned)
                turned = jnp.where(sub % 4 == 2, sroll(val, 5), turned)
                turned = jnp.where(sub % 4 == 3, sroll(val, 7), turned)
                old = outs[f][z, size_x - SUBL : size_x, :]
                outs[f][z, size_x - SUBL : size_x, :] = old + wt * (turned - old)
            return carry

        lax.fori_loop(0, ZC, body, 0)

    per = SUBL // xs

    def side_blend(pieces, first, dist):
        wts = []
        for b in range(blocks):
            rt = rate[SUBL * b : SUBL * (b + 1), :].astype(F32)
            wts.append(jnp.maximum(rt - dist, 0.0) / rt)

        def body(z, carry):
            t, c = z // 10, z % 10
            shift = jnp.mod(first - GROUP * c + LANES, LANES)
            for f in range(3):
                for b in range(blocks):
                    val = pieces[b * per][0, f, t]
                    for s in range(1, per):
                        val = jnp.where(sub // xs == s, pieces[b * per + s][0, f, t], val)
                    val = pltpu.roll(val, shift, 1)
                    old = outs[f][z, SUBL * b : SUBL * (b + 1), :]
                    outs[f][z, SUBL * b : SUBL * (b + 1), :] = old + wts[b] * (val - old)
            return carry

        lax.fori_loop(0, ZC, body, 0)

    @pl.when(gy == 0)
    def _():
        pieces = [sn_own[0]] + [sn_in[s - 1] for s in range(1, n_gy)]
        side_blend(pieces, 0, lane.astype(F32))

    @pl.when(gy == n_gy - 1)
    def _():
        pieces = [sn_in[n_gy - 2 - s] for s in range(n_gy - 1)] + [sn_own[1]]
        side_blend(pieces, LANES - band, (LANES - 1 - lane).astype(F32))

    even = (gx % 2) == 0
    top = size_x - SUBL

    def strip_of(blocks_of):
        acc = jnp.zeros((SUBL, LANES), F32)
        for b in range(blocks):
            lo = GROUP * (b + 1)
            moved = lroll(blocks_of(b), lo + DEEP)
            acc = jnp.where((lane >= lo) & (lane < lo + GROUP), moved, acc)
        return acc

    def corner_of(strip, spot, acc):
        o = 2 * GROUP * spot
        acc = jnp.where((lane >= o) & (lane < o + GROUP), lroll(strip, o - GROUP * blocks), acc)
        return jnp.where(
            (lane >= o + GROUP) & (lane < o + 2 * GROUP), lroll(strip, o), acc
        )

    def body(h, carry):
        corners = [jnp.zeros((SUBL, LANES), F32)] * 4
        for c5 in range(5):
            z = h * 5 + c5
            for f, src in enumerate((ub, vb, pb, w)):
                strip = strip_of(lambda b: src[z, SUBL * b : SUBL * (b + 1), :])
                q[0, f * ZC + z] = strip
                corners[f] = corner_of(strip, c5, corners[f])
            u7 = ub[z, top:, :]
            u0 = ub[z, 0:SUBL, :]
            v7 = vb[z, top:, :]
            v0 = vb[z, 0:SUBL, :]
            up7 = ub[z, top - 1 : size_x - 1, :]
            up0 = jnp.where(sub == 0, 0.0, sroll(u0, 1))
            e7 = SPREAD * ((u7 - up7) + (v7 - jnp.where(lane == 0, 0.0, lroll(v7, 1))))
            e0 = SPREAD * ((u0 - up0) + (v0 - jnp.where(lane == 0, 0.0, lroll(v0, 1))))
            ea = jnp.where(sub < 2, sroll(e7, -3), pb[z, top:, :])
            eb = jnp.where(sub < 3, sroll(e7, -5), w[z, top:, :])
            wa = jnp.where(sub < 6, pb[z, 0:SUBL, :], sroll(e0, 6))
            wb = jnp.where(sub < 5, w[z, 0:SUBL, :], sroll(e0, 3))
            at = 2 * SUBL * c5
            xa[h, at : at + SUBL, :] = jnp.where(even, ea, wa)
            xa[h, at + SUBL : at + 2 * SUBL, :] = jnp.where(even, eb, wb)
            xb[h, at : at + SUBL, :] = jnp.where(even, wa, ea)
            xb[h, at + SUBL : at + 2 * SUBL, :] = jnp.where(even, wb, eb)
            last = ub[z, size_x - 1 : size_x, :]
            xa[h, 80 + c5 : 81 + c5, :] = last
            xb[h, 80 + c5 : 81 + c5, :] = last
        for f in range(4):
            c_out[0, f * (ZC // 5) + h] = corners[f]
        return carry

    lax.fori_loop(0, ZC // 5, body, 0)
    strip = strip_of(lambda b: r[SUBL * b : SUBL * (b + 1), :])
    q[0, 4 * ZC] = strip
    c_out[0, 4 * (ZC // 5)] = corner_of(strip, 0, jnp.zeros((SUBL, LANES), F32))
    east_r = r[size_x - 5 : size_x, :]
    west_r = r[0:5, :]
    ra = jnp.where(even, east_r, west_r)
    rb = jnp.where(even, west_r, east_r)
    for ref, val in ((xa, ra), (xb, rb)):
        ref[0, 85:88, :] = val[0:3]
        ref[1, 85:87, :] = val[3:5]
        ref[1, 87:88, :] = val[4:5]
        ref[2, 85:88, :] = val[0:3]
        ref[3, 85:88, :] = val[0:3]


def substeps(n_gx, n_gy, *refs):
    (ub, vb, pb, w, r, xa, xb, qa, qb, ca, cb, caa, cab, cba, cbb) = refs[:15]
    (u_out, v_out, w_out, p_out) = refs[15:19]
    (PM, EM, WM, GM, QM, SM, PS, ES, WS, GS, QS, SS, RM) = refs[19:]
    levels, size_x = ub.shape[0], ub.shape[1]
    blocks = size_x // SUBL
    full = blocks + 2
    gx = lax.axis_index("gx")
    gy = lax.axis_index("gy")
    x_even = (gx % 2) == 0
    y_even = (gy % 2) == 0
    is_w, is_e = gx == 0, gx == n_gx - 1
    is_s, is_n = gy == 0, gy == n_gy - 1
    lane = lane_ids()
    sub = sub_ids()
    within = lane % GROUP
    block_of = lane // GROUP
    low_half = within < DEEP
    own_rows = (block_of >= 1) & (block_of <= blocks)
    zero = jnp.zeros((SUBL, LANES), F32)

    def strip_from(qs, qn, cw, ce, spot):
        o = 2 * GROUP * spot
        mine = jnp.where(low_half, qs, qn)
        got = jnp.where(block_of == 0, pltpu.roll(cw, jnp.mod(LANES - o, LANES), 1), mine)
        return jnp.where(
            block_of == full - 1,
            pltpu.roll(ce, jnp.mod(LANES + GROUP * blocks - o, LANES), 1),
            got,
        )

    def four(k, i):
        aa, ab, ba, bb = caa[k, i], cab[k, i], cba[k, i], cbb[k, i]
        xa_ya = jnp.where(y_even, ab, aa)
        xa_yb = jnp.where(y_even, aa, ab)
        xb_ya = jnp.where(y_even, bb, ba)
        xb_yb = jnp.where(y_even, ba, bb)
        sw = jnp.where(x_even, xb_ya, xa_ya)
        nw = jnp.where(x_even, xb_yb, xa_yb)
        se = jnp.where(x_even, xa_ya, xb_ya)
        ne = jnp.where(x_even, xa_yb, xb_yb)
        return jnp.where(low_half, sw, nw), jnp.where(low_half, se, ne)

    def strip_at(k, iq, ic, spot):
        a, b = qa[k, iq], qb[k, iq]
        cw, ce = four(k, ic)
        return strip_from(jnp.where(y_even, b, a), jnp.where(y_even, a, b), cw, ce, spot)

    def xneigh(s):
        up = sroll(s, 1)
        up = jnp.where(sub == 0, lroll(up, GROUP), up)
        dn = sroll(s, -1)
        dn = jnp.where(sub == SUBL - 1, lroll(dn, -GROUP), dn)
        return up, dn

    def edge_pack(tiles):
        acc = zero
        for b, tile in tiles:
            lo = GROUP * b + DEEP
            acc = jnp.where((lane == lo) | (lane == lo - 1), lroll(tile, lo), acc)
        return acc

    rims = ((within == DEEP - 1), (within == DEEP))

    def fix_main(tiles):
        first = jnp.where(is_w & (sub == SUBL - 1), sroll(tiles[1], -1), tiles[0])
        last = jnp.where(is_e & (sub == 0), 0.0, tiles[full - 1])
        return [first] + tiles[1:-1] + [last]

    def fix_strip_x(s):
        _, dn = xneigh(s)
        s = jnp.where(is_w & (block_of == 0) & (sub == SUBL - 1), dn, s)
        return jnp.where(is_e & (block_of == full - 1) & (sub == 0), 0.0, s)

    for b in range(blocks):
        RM[SUBL * (b + 1) : SUBL * (b + 2), :] = r[SUBL * b : SUBL * (b + 1), :]
    west_x = lambda h, lo, hi: jnp.where(x_even, xb[h, lo:hi, :], xa[h, lo:hi, :])
    east_x = lambda h, lo, hi: jnp.where(x_even, xa[h, lo:hi, :], xb[h, lo:hi, :])
    RM[0:SUBL, :] = jnp.ones((SUBL, LANES), F32)
    RM[SUBL * (full - 1) : SUBL * full, :] = jnp.ones((SUBL, LANES), F32)
    RM[3:6, :] = west_x(0, 85, 88)
    RM[6:8, :] = west_x(1, 85, 87)
    lo = SUBL * (full - 1)
    RM[lo : lo + 3, :] = east_x(0, 85, 88)
    RM[lo + 3 : lo + 5, :] = east_x(1, 85, 87)
    coefs = [RM[SUBL * b : SUBL * (b + 1), :] for b in range(full)]
    coefs.append(strip_at(0, 4 * ZC, 4 * (ZC // 5), 0))
    coefs = [jnp.where(c > 0.0, c, 1.0) for c in coefs]
    RM[SUBL * full :, :] = coefs[-1]
    for b in range(full):
        RM[SUBL * b : SUBL * (b + 1), :] = coefs[b]
    kappas = [2.0 * c / ((1.0 + 2.0 * c) + jnp.sqrt(1.0 + 4.0 * c)) for c in coefs]
    rhos = [k * k for k in kappas]

    def factor_body(z, carry):
        powers, lows = carry
        new_p, new_l = [], []
        for b in range(full + 1):
            nxt = powers[b] * rhos[b]
            high = 1.0 - nxt
            g = kappas[b] * (lows[b] / high)
            if b < full:
                GM[z, SUBL * b : SUBL * (b + 1), :] = g
            else:
                GS[z] = g
            new_p.append(nxt)
            new_l.append(high)
        return tuple(new_p), tuple(new_l)

    lax.fori_loop(
        0, levels, factor_body, (tuple(rhos), tuple(1.0 - x for x in rhos))
    )

    def unpack(z, carry):
        k, zz = z // ZC, z % ZC
        h, c5 = z // 5, z % 5
        s5 = ZC // 5
        hh = zz // 5
        strips = []
        for f in range(4):
            strips.append(strip_at(k, f * ZC + zz, f * s5 + hh, c5))
        us, vs, ps, ws = strips
        at = pl.multiple_of(2 * SUBL * c5, SUBL)
        xa_a, xa_b = xa[h, pl.ds(at, SUBL), :], xa[h, pl.ds(at + SUBL, SUBL), :]
        xb_a, xb_b = xb[h, pl.ds(at, SUBL), :], xb[h, pl.ds(at + SUBL, SUBL), :]
        wa, wb = jnp.where(x_even, xb_a, xa_a), jnp.where(x_even, xb_b, xa_b)
        ea, eb = jnp.where(x_even, xa_a, xb_a), jnp.where(x_even, xa_b, xb_b)
        e_west = jnp.where(sub < 5, sroll(wa, 3), sroll(wb, 5))
        e_east = jnp.where(sub < 2, sroll(ea, 2), sroll(eb, -3))
        u_row = jnp.where(
            x_even, xb[h, pl.ds(80 + c5, 1), :], xa[h, pl.ds(80 + c5, 1), :]
        )
        u_row = jnp.where(is_w, 0.0, u_row)
        o = 2 * GROUP * c5
        i_v = s5 + hh
        cw = jnp.where(x_even, cb[k, i_v], ca[k, i_v])
        ce = jnp.where(x_even, ca[k, i_v], cb[k, i_v])
        vm = [vb[z, SUBL * b : SUBL * (b + 1), :] for b in range(blocks)]
        vpack = edge_pack([(b + 1, vm[b]) for b in range(blocks)])
        vpack = jnp.where(block_of == 0, pltpu.roll(cw, jnp.mod(LANES - o, LANES), 1), vpack)
        vpack = jnp.where(
            block_of == full - 1,
            pltpu.roll(ce, jnp.mod(LANES + GROUP * blocks - o, LANES), 1),
            vpack,
        )
        u_up, _ = xneigh(us)
        v_left = jnp.where(within == DEEP, lroll(vpack, 1), lroll(vs, 1))
        es = SPREAD * ((us - u_up) + (vs - v_left))
        ES[z] = es
        ps = fix_strip_x(ps)
        PS[z] = ps
        WS[z] = ws
        SS[z] = zero
        tiles = [wa] + [pb[z, SUBL * b : SUBL * (b + 1), :] for b in range(blocks)] + [ea]
        tiles = fix_main(tiles)
        for b in range(full):
            PM[z, SUBL * (b + 1) : SUBL * (b + 2), :] = tiles[b]
            v_rim = jnp.where(lane == 0, lroll(vs, -(GROUP * b + DEEP - 1)), 0.0)
            if b == 0:
                e = e_west - SPREAD * v_rim
                ww = wb
            elif b == full - 1:
                u63 = jnp.where(sub == 0, sroll(ub[z, size_x - SUBL :, :], 1), 0.0)
                e = e_east - SPREAD * (v_rim + u63)
                ww = eb
            else:
                m = b - 1
                uu = ub[z, SUBL * m : SUBL * (m + 1), :]
                if m == 0:
                    up = jnp.where(sub == 0, u_row, sroll(uu, 1))
                else:
                    up = ub[z, SUBL * m - 1 : SUBL * (m + 1) - 1, :]
                left = jnp.where(lane == 0, v_rim, lroll(vm[m], 1))
                e = SPREAD * ((uu - up) + (vm[m] - left))
                ww = w[z, SUBL * m : SUBL * (m + 1), :]
                SM[z, SUBL * m : SUBL * (m + 1), :] = zero
            EM[z, SUBL * b : SUBL * (b + 1), :] = e
            WM[z, SUBL * b : SUBL * (b + 1), :] = ww
        SM[z, size_x:, :] = zero
        PM[z, 0:SUBL, :] = zero
        PM[z, SUBL * (full + 1) :, :] = zero
        return carry

    lax.fori_loop(0, levels, unpack, 0)

    rinvs = lambda b: RM[SUBL * b : SUBL * (b + 1), :]
    for b in range(full + 1):
        RM[SUBL * b : SUBL * (b + 1), :] = 1.0 / RM[SUBL * b : SUBL * (b + 1), :]

    coef_step = ACCEL * SPREAD

    def step(_, carry):
        def sections(z):
            qs = []
            ps = PS[z]
            mains = [PM[z, SUBL * (b + 1) : SUBL * (b + 2), :] for b in range(full)]
            cpack = edge_pack(list(enumerate(mains)))
            ps = jnp.where(is_s & rims[0], lroll(cpack, -1), ps)
            ps = jnp.where(is_n & rims[1], 0.0, ps)
            for b in range(full):
                p0 = mains[b]
                up = PM[z, SUBL * (b + 1) - 1 : SUBL * (b + 2) - 1, :]
                dn = PM[z, SUBL * (b + 1) + 1 : SUBL * (b + 2) + 1, :]
                t = lroll(ps, -(GROUP * b + DEEP))
                lf = lroll(jnp.where(lane == LANES - 1, t, p0), 1)
                rt = lroll(jnp.where(lane == 0, t, p0), -1)
                lap = ((lf + rt) + (up + dn)) - 4.0 * p0
                e = EM[z, SUBL * b : SUBL * (b + 1), :] - coef_step * lap
                EM[z, SUBL * b : SUBL * (b + 1), :] = e
                qq = p0 - e
                QM[z, SUBL * b : SUBL * (b + 1), :] = qq
                qs.append(qq)
                if b >= 1:
                    m = b - 1
                    SM[z, SUBL * m : SUBL * (m + 1), :] += p0
            up, dn = xneigh(ps)
            lf = jnp.where(rims[1], lroll(cpack, 1), lroll(ps, 1))
            rt = jnp.where(rims[0], lroll(cpack, -1), lroll(ps, -1))
            lap = ((lf + rt) + (up + dn)) - 4.0 * ps
            e = ES[z] - coef_step * lap
            ES[z] = e
            qq = ps - e
            QS[z] = qq
            SS[z] += ps
            qs.append(qq)
            return qs

        def eliminate(z, q_here, q_next, d_prev):
            ds = []
            for b in range(full + 1):
                if b < full:
                    sl = (z, slice(SUBL * b, SUBL * (b + 1)), slice(None))
                    wv, g = WM[sl], GM[sl]
                else:
                    wv, g = WS[z], GS[z]
                rhs = wv + BUOYANCY * (q_here[b] - q_next[b])
                d = g * (rhs * rinvs(b) + d_prev[b])
                if b < full:
                    WM[sl] = d
                else:
                    WS[z] = d
                ds.append(d)
            return ds

        def forward(z, carry):
            q_prev, d_prev = carry
            q_now = sections(z)
            ds = eliminate(z - 1, q_prev, q_now, d_prev)
            return tuple(q_now), tuple(ds)

        q0 = sections(0)
        zeros = tuple([zero] * (full + 1))
        q_last, d_last = lax.fori_loop(1, levels, forward, (tuple(q0), zeros))
        ds = eliminate(levels - 1, q_last, zeros, d_last)

        def finish(z, above, here):
            tiles = []
            for b in range(full + 1):
                qv = QM[z, SUBL * b : SUBL * (b + 1), :] if b < full else QS[z]
                tiles.append(qv - BUOYANCY * (above[b] - here[b]))
            mains = fix_main(tiles[:full])
            for b in range(full):
                PM[z, SUBL * (b + 1) : SUBL * (b + 2), :] = mains[b]
            PS[z] = fix_strip_x(tiles[full])

        def backward(i, above):
            z = levels - 2 - i
            here = []
            for b in range(full + 1):
                if b < full:
                    sl = (z, slice(SUBL * b, SUBL * (b + 1)), slice(None))
                    val = WM[sl] + GM[sl] * above[b]
                    WM[sl] = val
                else:
                    val = WS[z] + GS[z] * above[b]
                    WS[z] = val
                here.append(val)
            finish(z + 1, above, here)
            return tuple(here)

        bottom = lax.fori_loop(0, levels - 1, backward, tuple(ds))
        finish(0, bottom, zeros)
        return carry

    lax.fori_loop(0, SUBSTEPS, step, 0)

    def emit(z, carry):
        ss = SS[z]
        for m in range(blocks):
            rows = slice(SUBL * m, SUBL * (m + 1))
            s0 = SM[z, rows, :]
            dn = SM[z, SUBL * m + 1 : SUBL * (m + 1) + 1, :]
            t = lroll(ss, -(GROUP * (m + 1) + DEEP))
            rt = lroll(jnp.where(lane == 0, t, s0), -1)
            u_out[z, rows, :] = ub[z, rows, :] - ACCEL * (dn - s0)
            v_out[z, rows, :] = vb[z, rows, :] - ACCEL * (rt - s0)
            w_out[z, rows, :] = WM[z, SUBL * (m + 1) : SUBL * (m + 2), :]
            p_out[z, rows, :] = PM[z, SUBL * (m + 2) : SUBL * (m + 3), :]
        return carry

    lax.fori_loop(0, levels, emit, 0)


def swap(block, axis, second):
    n = lax.axis_size(axis)
    return lax.ppermute(block, axis, pairing(n, second))


def pairing(n, second):
    lo = 1 if second else 0
    pairs = []
    for i in range(lo, n - 1, 2):
        pairs += [(i, i + 1), (i + 1, i)]
    return pairs


def swap2(block, second_x, second_y):
    nx, ny = lax.axis_size("gx"), lax.axis_size("gy")
    pairs = []
    for a, b in pairing(nx, second_x):
        for c, d in pairing(ny, second_y):
            pairs.append((a * ny + c, b * ny + d))
    return lax.ppermute(block, ("gx", "gy"), pairs)


def to_ends(low, high, axis):
    n = lax.axis_size(axis)
    me = lax.axis_index(axis)
    got = []
    for k in range(1, n):
        block = jnp.where(me == k, low, high)
        got.append(lax.ppermute(block, axis, [(k, 0), (n - 1 - k, n - 1)]))
    return got


def per_device(u_wind, v_wind, w_wind, pressure, vert_coef, we_slab, sn_slab, relax_width):
    n_gx, n_gy = lax.axis_size("gx"), lax.axis_size("gy")
    levels, size_x, size_y = pressure.shape
    blocks = size_x // SUBL
    full = blocks + 2
    band, m = we_slab.shape[3], we_slab.shape[4]
    xs = sn_slab.shape[4]
    steps = levels // ZC
    sds = jax.ShapeDtypeStruct
    big = pltpu.CompilerParams(vmem_limit_bytes=60 * 1024 * 1024)

    sn_t = jnp.transpose(sn_slab, (0, 1, 2, 4, 3))
    we_shape = (steps, 3, ZC // 4, SUBL, LANES)
    sn_shape = (steps, 3, ZC // 10, SUBL, LANES)
    lead = lambda shape: pl.BlockSpec((1,) + shape[1:], lambda i: (i,) + (0,) * (len(shape) - 1))
    west, east, south, north = pl.pallas_call(
        pack_slabs,
        grid=(steps,),
        in_specs=[
            pl.BlockSpec((2, 3, ZC, band, m), lambda i: (0, 0, i, 0, 0)),
            pl.BlockSpec((2, 3, ZC, xs, band), lambda i: (0, 0, i, 0, 0)),
        ],
        out_specs=[lead(we_shape)] * 2 + [lead(sn_shape)] * 2,
        out_shape=[sds(we_shape, F32)] * 2 + [sds(sn_shape, F32)] * 2,
        name="pack_slabs",
    )(we_slab, sn_t)
    we_in = to_ends(west, east, "gx")
    sn_in = to_ends(south, north, "gy")

    field = pl.BlockSpec((ZC, size_x, size_y), lambda i: (i, 0, 0))
    plane = pl.BlockSpec((size_x, size_y), lambda i: (0, 0))
    x_shape = (levels // 5, 88, LANES)
    q_shape = (steps, 4 * ZC + 1, SUBL, LANES)
    c_shape = (steps, 4 * (ZC // 5) + 1, SUBL, LANES)
    ub, vb, pb, xa, xb, q, c = pl.pallas_call(
        functools.partial(blend_pack, n_gx, n_gy, m, xs, band),
        grid=(steps,),
        in_specs=[field] * 4
        + [plane] * 2
        + [lead(we_shape)] * 2
        + [lead(sn_shape)] * 2
        + [lead(we_shape)] * (n_gx - 1)
        + [lead(sn_shape)] * (n_gy - 1),
        out_specs=[field] * 3
        + [pl.BlockSpec((ZC // 5, 88, LANES), lambda i: (i, 0, 0))] * 2
        + [lead(q_shape), lead(c_shape)],
        out_shape=[sds(pressure.shape, F32)] * 3
        + [sds(x_shape, F32)] * 2
        + [sds(q_shape, F32), sds(c_shape, F32)],
        compiler_params=big,
        name="blend_pack",
    )(
        u_wind, v_wind, pressure, w_wind, vert_coef, relax_width,
        west, east, south, north, *we_in, *sn_in,
    )
    xa = swap(xa, "gx", False)
    xb = swap(xb, "gx", True)
    qa = swap(q, "gy", False)
    qb = swap(q, "gy", True)
    ca = swap(c, "gx", False)
    cb = swap(c, "gx", True)
    caa = swap2(c, False, False)
    cab = swap2(c, False, True)
    cba = swap2(c, True, False)
    cbb = swap2(c, True, True)

    whole = pl.BlockSpec(memory_space=pltpu.VMEM)
    tall = pltpu.VMEM((levels, SUBL * full, LANES), F32)
    strip = pltpu.VMEM((levels, SUBL, LANES), F32)
    return pl.pallas_call(
        functools.partial(substeps, n_gx, n_gy),
        in_specs=[whole] * 15,
        out_specs=[whole] * 4,
        out_shape=[sds(pressure.shape, F32)] * 4,
        scratch_shapes=[
            pltpu.VMEM((levels, SUBL * (full + 2), LANES), F32),
            tall, tall, tall, tall,
            pltpu.VMEM((levels, SUBL * (blocks + 1), LANES), F32),
            strip, strip, strip, strip, strip, strip,
            pltpu.VMEM((SUBL * (full + 1), LANES), F32),
        ],
        compiler_params=big,
        name="substeps",
    )(ub, vb, pb, w_wind, vert_coef, xa, xb, qa, qb, ca, cb, caa, cab, cba, cbb)


def solution(mesh):
    cell = P(None, "gx", "gy")
    placed = (
        cell, cell, cell, cell,
        P("gx", "gy"),
        P(None, None, None, None, ("gy", "gx")),
        P(None, None, None, None, ("gx", "gy")),
        P("gx", "gy"),
    )
    return jax.shard_map(
        per_device,
        mesh=mesh,
        in_specs=placed,
        out_specs=(cell, cell, cell, cell),
        check_vma=False,
    )
```

profile of v0, /device:TPU:10, one launch (start us, length us, event | category | flops | bytes accessed | tf_op | source)
XLA Modules:
  0.0 296.8 jit_solution(3485939751059270194)
XLA Ops:
  0.7 2.7 copy.13.we
  3.4 1.7 copy.12
  5.1 4.2 %pack_slabs.1 = (f32[3,3,5,8,128]{4,3,2,1,0:T(8,128)}, f32[3,3,5,8,128]{4,3,2,1,0:T(8,128)}, f32[3,3,2,8,128]{4,3,2,1,0:T(8,128)}, f32[3,3,2,8,128]{4,3,2,1,0:T(8,128)}) custom-call(f32[2,3,60,5,32]{4,3,2,1,0:T(8,128)} %copy.13.we, f32[2,3,60,8,5]{4,3,2,1,0:T(8,128)} %bitcast.1), custom_call_target="tpu_custom_call" | custom-call | tf_op jit(solution)/shard_map/pack_slabs/pallas_call | solution.py:574
  9.3 1.0 broadcast_select_fusion.3
  10.3 0.7 collective-permute-start.9
  11.0 0.7 collective-permute-start.8
  11.6 6.3 %collective-permute-start.7 = (f32[3,3,2,8,128]{4,3,2,1,0:T(8,128)S(1)}, f32[3,3,2,8,128]{4,3,2,1,0:T(8,128)S(1)}, u32[]{:S(2)}, u32[]{:S(2)}) collective-permute-start(f32[3,3,2,8,128]{4,3,2,1,0:T(8,128)S(1)} %get-tuple-element.31), channel_id=1, source_target_pairs={{5,0},{2,7},{13,8},{10,15},{21,16},{18,23},{29,24},{26,31}} | collective-permute-start | bytes 221192 | tf_op jit(solution)/shard_map/ppermute | solution.py:555
  18.0 1.1 broadcast_select_fusion
  19.0 0.7 collective-permute-start.2
  19.7 4.7 %collective-permute-start.1 = (f32[3,3,5,8,128]{4,3,2,1,0:T(8,128)S(1)}, f32[3,3,5,8,128]{4,3,2,1,0:T(8,128)S(1)}, u32[]{:S(2)}, u32[]{:S(2)}) collective-permute-start(f32[3,3,5,8,128]{4,3,2,1,0:T(8,128)S(1)} %get-tuple-element.27), channel_id=1, source_target_pairs={{16,0},{8,24},{17,1},{9,25},{18,2},{10,26},{19,3},{11,27},{20,4},{... | collective-permute-start | bytes 552968 | tf_op jit(solution)/shard_map/ppermute | solution.py:555
  24.4 2.7 collective-permute-start
  27.2 0.7 collective-permute-start.6
  27.9 0.7 collective-permute-start.5
  28.6 8.1 %collective-permute-start.4 = (f32[3,3,2,8,128]{4,3,2,1,0:T(8,128)S(1)}, f32[3,3,2,8,128]{4,3,2,1,0:T(8,128)S(1)}, u32[]{:S(2)}, u32[]{:S(2)}) collective-permute-start(f32[3,3,2,8,128]{4,3,2,1,0:T(8,128)S(1)} %get-tuple-element.34), channel_id=1, source_target_pairs={{2,0},{5,7},{10,8},{13,15},{18,16},{21,23},{26,24},{29,31}} | collective-permute-start | bytes 221192 | tf_op jit(solution)/shard_map/ppermute | solution.py:555
  36.7 0.7 collective-permute-start.3
  37.4 1.3 collective-permute-done.4.refs_14_
  38.7 0.5 copy-done.19
  39.4 0.7 copy-done.12
  40.1 13.7 %blend_pack.1 = (f32[60,64,128]{2,1,0:T(8,128)}, f32[60,64,128]{2,1,0:T(8,128)}, f32[60,64,128]{2,1,0:T(8,128)}, f32[12,88,128]{2,1,0:T(8,128)}, f32[12,88,128]{...) custom-call(f32[60,64,128]{2,1,0:T(8,128)} %refs_0_.1, f32[60,64,128]{2,1,0:T(8,128)} %refs_1_.1, ...), custom_call_target="tpu_custom_call" | custom-call | tf_op jit(solution)/shard_map/blend_pack/pallas_call | solution.py:593
  53.8 2.2 collective-permute-start.13
  56.1 10.0 %collective-permute-start.19 = (f32[3,17,8,128]{3,2,1,0:T(8,128)}, f32[3,17,8,128]{3,2,1,0:T(8,128)S(1)}, u32[]{:S(2)}, u32[]{:S(2)}) collective-permute-start(f32[3,17,8,128]{3,2,1,0:T(8,128)} %get-tuple-element.25), channel_id=1, source_target_pairs={{9,18},{10,17},{11,20},{12,19},{13,22},{14,21},{17,10},{18,9},{19,... | collective-permute-start | bytes 626696 | tf_op jit(solution)/shard_map/ppermute | solution.py:546
  66.1 1.9 collective-permute-start.18
  68.0 2.8 collective-permute-start.17
  70.8 2.5 collective-permute-done.19.refs_14_
  73.3 8.4 %collective-permute-done.18.refs_13_ = f32[3,17,8,128]{3,2,1,0:T(8,128)S(1)} collective-permute-done((f32[3,17,8,128]{3,2,1,0:T(8,128)}, f32[3,17,8,128]{3,2,1,0:T(8,128)S(1)}, u32[]{:S(2)}, u32[]{:S(2)}) %collective-permute-start.18) | collective-permute-done | bytes 208928 | tf_op jit(solution)/shard_map/ppermute | solution.py:546
  81.7 3.4 %collective-permute-start.11 = (f32[12,88,128]{2,1,0:T(8,128)}, f32[12,88,128]{2,1,0:T(8,128)S(1)}, u32[]{:S(2)}, u32[]{:S(2)}) collective-permute-start(f32[12,88,128]{2,1,0:T(8,128)} %get-tuple-element.23), channel_id=1, source_target_pairs={{8,16},{16,8},{9,17},{17,9},{10,18},{18,10},{11,19},{19,11},{12,20... | collective-permute-start | bytes 1622024 | tf_op jit(solution)/shard_map/ppermute | solution.py:529
  85.1 3.4 %collective-permute-start.15 = (f32[3,17,8,128]{3,2,1,0:T(8,128)}, f32[3,17,8,128]{3,2,1,0:T(8,128)S(1)}, u32[]{:S(2)}, u32[]{:S(2)}) collective-permute-start(f32[3,17,8,128]{3,2,1,0:T(8,128)} %get-tuple-element.25), channel_id=1, source_target_pairs={{8,16},{16,8},{9,17},{17,9},{10,18},{18,10},{11,19},{19,11},{12,20... | collective-permute-start | bytes 626696 | tf_op jit(solution)/shard_map/ppermute | solution.py:529
  88.5 25.2 %collective-permute-done.15.refs_10_ = f32[3,17,8,128]{3,2,1,0:T(8,128)S(1)} collective-permute-done((f32[3,17,8,128]{3,2,1,0:T(8,128)}, f32[3,17,8,128]{3,2,1,0:T(8,128)S(1)}, u32[]{:S(2)}, u32[]{:S(2)}) %collective-permute-start.15) | collective-permute-done | bytes 208928 | tf_op jit(solution)/shard_map/ppermute | solution.py:529
  113.7 7.4 %collective-permute-done.14.refs_9_ = f32[3,17,8,128]{3,2,1,0:T(8,128)S(1)} collective-permute-done((f32[3,17,8,128]{3,2,1,0:T(8,128)}, f32[3,17,8,128]{3,2,1,0:T(8,128)S(1)}, u32[]{:S(2)}, u32[]{:S(2)}) %collective-permute-start.14) | collective-permute-done | bytes 208928 | tf_op jit(solution)/shard_map/ppermute | solution.py:529
  121.1 0.6 copy-done.9
  122.5 0.3 copy-done.1
  122.8 174.0 %substeps.1 = (f32[60,64,128]{2,1,0:T(8,128)}, f32[60,64,128]{2,1,0:T(8,128)}, f32[60,64,128]{2,1,0:T(8,128)}, f32[60,64,128]{2,1,0:T(8,128)}) custom-call(f32[60,64,128]{2,1,0:T(8,128)} %get-tuple-element.19.refs_0_, f32[60,64,128]{2,1,0:T(8,128)} %get-tuple-element.20.refs_1_, f32[60,64,128]{2,1,0:T(8,128)} %get-tuple-element.21.refs_2_, ...), custom_call_target="tpu_custom_call" | custom-call | tf_op jit(solution)/shard_map/substeps/pallas_call | solution.py:628
  (57 shorter events, 1.0 us)
Async XLA Ops:
  0.6 2.8 copy-start.13
  10.3 14.1 %collective-permute-start.9 = (f32[3,3,2,8,128]{4,3,2,1,0:T(8,128)S(1)}, f32[3,3,2,8,128]{4,3,2,1,0:T(8,128)S(1)}, u32[]{:S(2)}, u32[]{:S(2)}) collective-permute-start(f32[3,3,2,8,128]{4,3,2,1,0:T(8,128)S(1)} %get-tuple-element.29), channel_id=1, source_target_pairs={{7,0},{0,7},{15,8},{8,15},{23,16},{16,23},{31,24},{24,31}} | collective-permute-start | bytes 221192 | tf_op jit(solution)/shard_map/ppermute | solution.py:555
  11.0 16.2 %collective-permute-start.8 = (f32[3,3,2,8,128]{4,3,2,1,0:T(8,128)S(1)}, f32[3,3,2,8,128]{4,3,2,1,0:T(8,128)S(1)}, u32[]{:S(2)}, u32[]{:S(2)}) collective-permute-start(f32[3,3,2,8,128]{4,3,2,1,0:T(8,128)S(1)} %get-tuple-element.30), channel_id=1, source_target_pairs={{6,0},{1,7},{14,8},{9,15},{22,16},{17,23},{30,24},{25,31}} | collective-permute-start | bytes 221192 | tf_op jit(solution)/shard_map/ppermute | solution.py:555
  11.6 16.2 %collective-permute-start.7 = (f32[3,3,2,8,128]{4,3,2,1,0:T(8,128)S(1)}, f32[3,3,2,8,128]{4,3,2,1,0:T(8,128)S(1)}, u32[]{:S(2)}, u32[]{:S(2)}) collective-permute-start(f32[3,3,2,8,128]{4,3,2,1,0:T(8,128)S(1)} %get-tuple-element.31), channel_id=1, source_target_pairs={{5,0},{2,7},{13,8},{10,15},{21,16},{18,23},{29,24},{26,31}} | collective-permute-start | bytes 221192 | tf_op jit(solution)/shard_map/ppermute | solution.py:555
  19.0 19.6 %collective-permute-start.2 = (f32[3,3,5,8,128]{4,3,2,1,0:T(8,128)S(1)}, f32[3,3,5,8,128]{4,3,2,1,0:T(8,128)S(1)}, u32[]{:S(2)}, u32[]{:S(2)}) collective-permute-start(f32[3,3,5,8,128]{4,3,2,1,0:T(8,128)S(1)} %get-tuple-element.26), channel_id=1, source_target_pairs={{24,0},{0,24},{25,1},{1,25},{26,2},{2,26},{27,3},{3,27},{28,4},{4,... | collective-permute-start | bytes 552968 | tf_op jit(solution)/shard_map/ppermute | solution.py:555
  19.7 19.0 %collective-permute-start.1 = (f32[3,3,5,8,128]{4,3,2,1,0:T(8,128)S(1)}, f32[3,3,5,8,128]{4,3,2,1,0:T(8,128)S(1)}, u32[]{:S(2)}, u32[]{:S(2)}) collective-permute-start(f32[3,3,5,8,128]{4,3,2,1,0:T(8,128)S(1)} %get-tuple-element.27), channel_id=1, source_target_pairs={{16,0},{8,24},{17,1},{9,25},{18,2},{10,26},{19,3},{11,27},{20,4},{... | collective-permute-start | bytes 552968 | tf_op jit(solution)/shard_map/ppermute | solution.py:555
  24.4 14.3 %copy-start.14 = (f32[3,3,2,8,128]{4,3,2,1,0:T(8,128)}, f32[3,3,2,8,128]{4,3,2,1,0:T(8,128)S(1)}, u32[]{:S(2)}) copy-start(f32[3,3,2,8,128]{4,3,2,1,0:T(8,128)S(1)} %collective-permute-done.9.refs_19_) | copy-start | bytes 221188
  24.4 14.3 %collective-permute-start = (f32[3,3,5,8,128]{4,3,2,1,0:T(8,128)S(1)}, f32[3,3,5,8,128]{4,3,2,1,0:T(8,128)S(1)}, u32[]{:S(2)}, u32[]{:S(2)}) collective-permute-start(f32[3,3,5,8,128]{4,3,2,1,0:T(8,128)S(1)} %get-tuple-element.28), channel_id=1, source_target_pairs={{8,0},{16,24},{9,1},{17,25},{10,2},{18,26},{11,3},{19,27},{12,4},{... | collective-permute-start | bytes 552968 | tf_op jit(solution)/shard_map/ppermute | solution.py:555
  27.2 11.5 %copy-start.15 = (f32[3,3,2,8,128]{4,3,2,1,0:T(8,128)}, f32[3,3,2,8,128]{4,3,2,1,0:T(8,128)S(1)}, u32[]{:S(2)}) copy-start(f32[3,3,2,8,128]{4,3,2,1,0:T(8,128)S(1)} %collective-permute-done.8.refs_18_) | copy-start | bytes 221188
  27.2 1.4 collective-permute-start.6
  27.9 10.8 %copy-start.16 = (f32[3,3,2,8,128]{4,3,2,1,0:T(8,128)}, f32[3,3,2,8,128]{4,3,2,1,0:T(8,128)S(1)}, u32[]{:S(2)}) copy-start(f32[3,3,2,8,128]{4,3,2,1,0:T(8,128)S(1)} %collective-permute-done.7.refs_17_) | copy-start | bytes 221188
  27.9 8.8 %collective-permute-start.5 = (f32[3,3,2,8,128]{4,3,2,1,0:T(8,128)S(1)}, f32[3,3,2,8,128]{4,3,2,1,0:T(8,128)S(1)}, u32[]{:S(2)}, u32[]{:S(2)}) collective-permute-start(f32[3,3,2,8,128]{4,3,2,1,0:T(8,128)S(1)} %get-tuple-element.33), channel_id=1, source_target_pairs={{3,0},{4,7},{11,8},{12,15},{19,16},{20,23},{27,24},{28,31}} | collective-permute-start | bytes 221192 | tf_op jit(solution)/shard_map/ppermute | solution.py:555
  28.5 10.2 %copy-start.17 = (f32[3,3,2,8,128]{4,3,2,1,0:T(8,128)}, f32[3,3,2,8,128]{4,3,2,1,0:T(8,128)S(1)}, u32[]{:S(2)}) copy-start(f32[3,3,2,8,128]{4,3,2,1,0:T(8,128)S(1)} %collective-permute-done.6.refs_16_) | copy-start | bytes 221188
  28.6 10.1 %collective-permute-start.4 = (f32[3,3,2,8,128]{4,3,2,1,0:T(8,128)S(1)}, f32[3,3,2,8,128]{4,3,2,1,0:T(8,128)S(1)}, u32[]{:S(2)}, u32[]{:S(2)}) collective-permute-start(f32[3,3,2,8,128]{4,3,2,1,0:T(8,128)S(1)} %get-tuple-element.34), channel_id=1, source_target_pairs={{2,0},{5,7},{10,8},{13,15},{18,16},{21,23},{26,24},{29,31}} | collective-permute-start | bytes 221192 | tf_op jit(solution)/shard_map/ppermute | solution.py:555
  36.7 2.0 copy-start.18
  36.7 1.9 collective-permute-start.3
  53.8 67.3 %collective-permute-start.13 = (f32[3,81,8,128]{3,2,1,0:T(8,128)}, f32[3,81,8,128]{3,2,1,0:T(8,128)S(1)}, u32[]{:S(2)}, u32[]{:S(2)}) collective-permute-start(f32[3,81,8,128]{3,2,1,0:T(8,128)} %get-tuple-element.24), channel_id=1, source_target_pairs={{1,2},{2,1},{3,4},{4,3},{5,6},{6,5},{9,10},{10,9},{11,12},{12,11},... | collective-permute-start | bytes 2985992 | tf_op jit(solution)/shard_map/ppermute | solution.py:529
  56.0 65.1 %collective-permute-start.12 = (f32[3,81,8,128]{3,2,1,0:T(8,128)}, f32[3,81,8,128]{3,2,1,0:T(8,128)S(1)}, u32[]{:S(2)}, u32[]{:S(2)}) collective-permute-start(f32[3,81,8,128]{3,2,1,0:T(8,128)} %get-tuple-element.24), channel_id=1, source_target_pairs={{0,1},{1,0},{2,3},{3,2},{4,5},{5,4},{6,7},{7,6},{8,9},{9,8},{10,11... | collective-permute-start | bytes 2985992 | tf_op jit(solution)/shard_map/ppermute | solution.py:529
  56.1 17.2 %collective-permute-start.19 = (f32[3,17,8,128]{3,2,1,0:T(8,128)}, f32[3,17,8,128]{3,2,1,0:T(8,128)S(1)}, u32[]{:S(2)}, u32[]{:S(2)}) collective-permute-start(f32[3,17,8,128]{3,2,1,0:T(8,128)} %get-tuple-element.25), channel_id=1, source_target_pairs={{9,18},{10,17},{11,20},{12,19},{13,22},{14,21},{17,10},{18,9},{19,... | collective-permute-start | bytes 626696 | tf_op jit(solution)/shard_map/ppermute | solution.py:546
  66.1 15.6 %collective-permute-start.18 = (f32[3,17,8,128]{3,2,1,0:T(8,128)}, f32[3,17,8,128]{3,2,1,0:T(8,128)S(1)}, u32[]{:S(2)}, u32[]{:S(2)}) collective-permute-start(f32[3,17,8,128]{3,2,1,0:T(8,128)} %get-tuple-element.25), channel_id=1, source_target_pairs={{8,17},{9,16},{10,19},{11,18},{12,21},{13,20},{14,23},{15,22},{16,... | collective-permute-start | bytes 626696 | tf_op jit(solution)/shard_map/ppermute | solution.py:546
  68.0 13.7 %collective-permute-start.17 = (f32[3,17,8,128]{3,2,1,0:T(8,128)}, f32[3,17,8,128]{3,2,1,0:T(8,128)S(1)}, u32[]{:S(2)}, u32[]{:S(2)}) collective-permute-start(f32[3,17,8,128]{3,2,1,0:T(8,128)} %get-tuple-element.25), channel_id=1, source_target_pairs={{1,10},{2,9},{3,12},{4,11},{5,14},{6,13},{9,2},{10,1},{11,4},{12,3... | collective-permute-start | bytes 626696 | tf_op jit(solution)/shard_map/ppermute | solution.py:546
  73.3 48.5 %copy-start.4 = (f32[3,17,8,128]{3,2,1,0:T(8,128)}, f32[3,17,8,128]{3,2,1,0:T(8,128)S(1)}, u32[]{:S(2)}) copy-start(f32[3,17,8,128]{3,2,1,0:T(8,128)S(1)} %collective-permute-done.19.refs_14_) | copy-start | bytes 626692
  73.3 11.8 %collective-permute-start.16 = (f32[3,17,8,128]{3,2,1,0:T(8,128)}, f32[3,17,8,128]{3,2,1,0:T(8,128)S(1)}, u32[]{:S(2)}, u32[]{:S(2)}) collective-permute-start(f32[3,17,8,128]{3,2,1,0:T(8,128)} %get-tuple-element.25), channel_id=1, source_target_pairs={{0,9},{1,8},{2,11},{3,10},{4,13},{5,12},{6,15},{7,14},{8,1},{9,0},... | collective-permute-start | bytes 626696 | tf_op jit(solution)/shard_map/ppermute | solution.py:546
  81.7 40.1 %copy-start.5 = (f32[3,17,8,128]{3,2,1,0:T(8,128)}, f32[3,17,8,128]{3,2,1,0:T(8,128)S(1)}, u32[]{:S(2)}) copy-start(f32[3,17,8,128]{3,2,1,0:T(8,128)S(1)} %collective-permute-done.18.refs_13_) | copy-start | bytes 626692
  81.7 39.4 %collective-permute-start.10 = (f32[12,88,128]{2,1,0:T(8,128)}, f32[12,88,128]{2,1,0:T(8,128)S(1)}, u32[]{:S(2)}, u32[]{:S(2)}) collective-permute-start(f32[12,88,128]{2,1,0:T(8,128)} %get-tuple-element.22), channel_id=1, source_target_pairs={{0,8},{8,0},{16,24},{24,16},{1,9},{9,1},{17,25},{25,17},{2,10},{10... | collective-permute-start | bytes 1622024 | tf_op jit(solution)/shard_map/ppermute | solution.py:529
  81.7 40.0 %copy-start.6 = (f32[3,17,8,128]{3,2,1,0:T(8,128)}, f32[3,17,8,128]{3,2,1,0:T(8,128)S(1)}, u32[]{:S(2)}) copy-start(f32[3,17,8,128]{3,2,1,0:T(8,128)S(1)} %collective-permute-done.17.refs_12_) | copy-start | bytes 626692
  81.7 39.3 %collective-permute-start.11 = (f32[12,88,128]{2,1,0:T(8,128)}, f32[12,88,128]{2,1,0:T(8,128)S(1)}, u32[]{:S(2)}, u32[]{:S(2)}) collective-permute-start(f32[12,88,128]{2,1,0:T(8,128)} %get-tuple-element.23), channel_id=1, source_target_pairs={{8,16},{16,8},{9,17},{17,9},{10,18},{18,10},{11,19},{19,11},{12,20... | collective-permute-start | bytes 1622024 | tf_op jit(solution)/shard_map/ppermute | solution.py:529
  85.1 36.7 %copy-start.7 = (f32[3,17,8,128]{3,2,1,0:T(8,128)}, f32[3,17,8,128]{3,2,1,0:T(8,128)S(1)}, u32[]{:S(2)}) copy-start(f32[3,17,8,128]{3,2,1,0:T(8,128)S(1)} %collective-permute-done.16.refs_11_) | copy-start | bytes 626692
  85.1 28.6 %collective-permute-start.15 = (f32[3,17,8,128]{3,2,1,0:T(8,128)}, f32[3,17,8,128]{3,2,1,0:T(8,128)S(1)}, u32[]{:S(2)}, u32[]{:S(2)}) collective-permute-start(f32[3,17,8,128]{3,2,1,0:T(8,128)} %get-tuple-element.25), channel_id=1, source_target_pairs={{8,16},{16,8},{9,17},{17,9},{10,18},{18,10},{11,19},{19,11},{12,20... | collective-permute-start | bytes 626696 | tf_op jit(solution)/shard_map/ppermute | solution.py:529
  113.7 8.1 %copy-start.8 = (f32[3,17,8,128]{3,2,1,0:T(8,128)}, f32[3,17,8,128]{3,2,1,0:T(8,128)S(1)}, u32[]{:S(2)}) copy-start(f32[3,17,8,128]{3,2,1,0:T(8,128)S(1)} %collective-permute-done.15.refs_10_) | copy-start | bytes 626692
  113.7 7.4 %collective-permute-start.14 = (f32[3,17,8,128]{3,2,1,0:T(8,128)}, f32[3,17,8,128]{3,2,1,0:T(8,128)S(1)}, u32[]{:S(2)}, u32[]{:S(2)}) collective-permute-start(f32[3,17,8,128]{3,2,1,0:T(8,128)} %get-tuple-element.25), channel_id=1, source_target_pairs={{0,8},{8,0},{16,24},{24,16},{1,9},{9,1},{17,25},{25,17},{2,10},{10... | collective-permute-start | bytes 626696 | tf_op jit(solution)/shard_map/ppermute | solution.py:529
  121.1 1.4 copy-start
  (9 other events, 7.2 us)
where the time goes:
time: 297 us
  Pallas kernels  192 us (65%)
  starting transfers between devices  49.6 us (17%)
  waiting for transfers between devices  44.7 us (15%)
  local copies, waits for them, and re-layouts  7.55 us (3%)
    pallas_call x1, Pallas kernels, per_device(): pl.pallas_call(functools.partial(substeps, n_gx, n_gy), in_specs=[whole]...  174 us
    ppermute x6, waiting for transfers between devices, swap(): return lax.ppermute(block, axis, pairing(n, second))  32.6 us
    ppermute x10, starting transfers between devices, to_ends(): got.append(lax.ppermute(block, axis, [(k, 0), (n - 1 - k, n - 1)]))  25.8 us
    ppermute x4, starting transfers between devices, swap2(): return lax.ppermute(block, ('gx', 'gy'), pairs)  14.7 us
    pallas_call x1, Pallas kernels, per_device(): pl.pallas_call(functools.partial(blend_pack, n_gx, n_gy, m, xs, band), gr...  13.7 us
    ppermute x4, waiting for transfers between devices, swap2(): return lax.ppermute(block, ('gx', 'gy'), pairs)  10.9 us
    ppermute x6, starting transfers between devices, swap(): return lax.ppermute(block, axis, pairing(n, second))  9.06 us
    unnamed x44, local copies, waits for them, and re-layouts  7.55 us
  transfers between devices with their start and end apart: 20, of which 5 were waited for; matrix products, arithmetic and copies ran while one was open for 0% of the time, Pallas kernels for 0%

commit v1 on v0

v1 whole, which is shorter than its diff:
```python
import functools
import jax
import jax.numpy as jnp
from jax import lax
from jax.experimental import pallas as pl
from jax.experimental.pallas import tpu as pltpu
from jax.sharding import PartitionSpec as P

SUBSTEPS = 6
ACCEL = 0.3
SPREAD = 0.3
BUOYANCY = 0.5
UNIT = 1.0 / ACCEL
DEEP = 6
GROUP = 2 * DEEP
ZC = 20
SUBL = 8
LANES = 128
F32 = jnp.float32


def lane_ids():
    return lax.broadcasted_iota(jnp.int32, (SUBL, LANES), 1)


def sub_ids():
    return lax.broadcasted_iota(jnp.int32, (SUBL, LANES), 0)


def lroll(x, shift):
    if isinstance(shift, int):
        shift = shift % LANES
        if shift == 0:
            return x
    return pltpu.roll(x, shift, 1)


def sroll(x, shift):
    return pltpu.roll(x, shift % SUBL, 0)


def pack_slabs(we, sn, west, east, south, north):
    band, m = we.shape[3], we.shape[4]
    xs = sn.shape[3]
    west[...] = jnp.zeros_like(west)
    east[...] = jnp.zeros_like(east)
    south[...] = jnp.zeros_like(south)
    north[...] = jnp.zeros_like(north)
    for f in range(3):
        for z in range(ZC):
            g, c = divmod(z, 4)
            west[0, f, g, 0:band, m * c : m * (c + 1)] = we[0, f, z]
            east[0, f, g, 0:band, m * c : m * (c + 1)] = we[1, f, z]
            t, c = divmod(z, 10)
            lo = GROUP * c
            s_val = sn[0, f, z]
            n_val = sn[1, f, z]
            for rep in range(SUBL // xs):
                rows = slice(xs * rep, xs * (rep + 1))
                south[0, f, t, rows, lo : lo + band] = s_val
                for d in range(band):
                    at = lo + band - 1 - d
                    north[0, f, t, rows, at : at + 1] = n_val[:, d : d + 1]


def blend_pack(n_gx, n_gy, m, xs, band, *refs):
    u, v, p, w, r, rate = refs[:6]
    refs = refs[6:]
    we_own = refs[:2]
    sn_own = refs[2:4]
    we_in = refs[4 : 4 + n_gx - 1]
    sn_in = refs[3 + n_gx : 3 + n_gx + n_gy - 1]
    ub, vb, pb, xa, xb, q, c_out = refs[2 + n_gx + n_gy :]
    gx = lax.axis_index("gx")
    gy = lax.axis_index("gy")
    size_x = u.shape[1]
    blocks = size_x // SUBL
    outs = (ub, vb, pb)
    for src, dst in zip((u, v, p), outs):
        dst[...] = src[...]
    lane = lane_ids()
    sub = sub_ids()

    def band_rows(pieces, f, z):
        g, c = z // 4, z % 4
        val = jnp.zeros((SUBL, LANES), F32)
        for s, piece in enumerate(pieces):
            moved = pltpu.roll(piece[0, f, g], jnp.mod(m * s - m * c, LANES), 1)
            val = jnp.where((lane >= m * s) & (lane < m * (s + 1)), moved, val)
        return val

    @pl.when(gx == 0)
    def _():
        pieces = [we_own[0]] + [we_in[s - 1] for s in range(1, n_gx)]
        rt = rate[0:SUBL, :].astype(F32)
        wt = jnp.maximum(rt - sub.astype(F32), 0.0) / rt

        def body(h, carry):
            for z in [h * 4 + i for i in range(4)]:
                for f in range(3):
                    val = band_rows(pieces, f, z)
                    old = outs[f][z, 0:SUBL, :]
                    outs[f][z, 0:SUBL, :] = old + wt * (val - old)
            return carry

        lax.fori_loop(0, ZC // 4, body, 0)

    @pl.when(gx == n_gx - 1)
    def _():
        pieces = [we_in[n_gx - 2 - s] for s in range(n_gx - 1)] + [we_own[1]]
        rt = rate[size_x - SUBL : size_x, :].astype(F32)
        wt = jnp.maximum(rt - (SUBL - 1 - sub).astype(F32), 0.0) / rt

        def body(h, carry):
            for z in [h * 4 + i for i in range(4)]:
                for f in range(3):
                    val = band_rows(pieces, f, z)
                    turned = sroll(val, 1)
                    turned = jnp.where(sub % 4 == 1, sroll(val, 3), turned)
                    turned = jnp.where(sub % 4 == 2, sroll(val, 5), turned)
                    turned = jnp.where(sub % 4 == 3, sroll(val, 7), turned)
                    old = outs[f][z, size_x - SUBL : size_x, :]
                    outs[f][z, size_x - SUBL : size_x, :] = old + wt * (turned - old)
            return carry

        lax.fori_loop(0, ZC // 4, body, 0)

    per = SUBL // xs

    def side_blend(pieces, first, dist):
        wts = []
        for b in range(blocks):
            rt = rate[SUBL * b : SUBL * (b + 1), :].astype(F32)
            wts.append(jnp.maximum(rt - dist, 0.0) / rt)

        def body(h, carry):
            for z in [h * 5 + i for i in range(5)]:
                t, c = z // 10, z % 10
                shift = jnp.mod(first - GROUP * c + LANES, LANES)
                for f in range(3):
                    for b in range(blocks):
                        val = pieces[b * per][0, f, t]
                        for s in range(1, per):
                            val = jnp.where(sub // xs == s, pieces[b * per + s][0, f, t], val)
                        val = pltpu.roll(val, shift, 1)
                        old = outs[f][z, SUBL * b : SUBL * (b + 1), :]
                        outs[f][z, SUBL * b : SUBL * (b + 1), :] = old + wts[b] * (val - old)
            return carry

        lax.fori_loop(0, ZC // 5, body, 0)

    @pl.when(gy == 0)
    def _():
        pieces = [sn_own[0]] + [sn_in[s - 1] for s in range(1, n_gy)]
        side_blend(pieces, 0, lane.astype(F32))

    @pl.when(gy == n_gy - 1)
    def _():
        pieces = [sn_in[n_gy - 2 - s] for s in range(n_gy - 1)] + [sn_own[1]]
        side_blend(pieces, LANES - band, (LANES - 1 - lane).astype(F32))

    even = (gx % 2) == 0
    top = size_x - SUBL

    def strip_of(blocks_of):
        acc = jnp.zeros((SUBL, LANES), F32)
        for b in range(blocks):
            lo = GROUP * (b + 1)
            moved = lroll(blocks_of(b), lo + DEEP)
            acc = jnp.where((lane >= lo) & (lane < lo + GROUP), moved, acc)
        return acc

    def corner_of(strip, spot, acc):
        o = 2 * GROUP * spot
        acc = jnp.where((lane >= o) & (lane < o + GROUP), lroll(strip, o - GROUP * blocks), acc)
        return jnp.where(
            (lane >= o + GROUP) & (lane < o + 2 * GROUP), lroll(strip, o), acc
        )

    def body(h, carry):
        corners = [jnp.zeros((SUBL, LANES), F32)] * 4
        for c5 in range(5):
            z = h * 5 + c5
            for f, src in enumerate((ub, vb, pb, w)):
                strip = strip_of(lambda b: src[z, SUBL * b : SUBL * (b + 1), :])
                q[0, f * ZC + z] = strip
                corners[f] = corner_of(strip, c5, corners[f])
            u7 = ub[z, top:, :]
            u0 = ub[z, 0:SUBL, :]
            v7 = vb[z, top:, :]
            v0 = vb[z, 0:SUBL, :]
            up7 = ub[z, top - 1 : size_x - 1, :]
            up0 = jnp.where(sub == 0, 0.0, sroll(u0, 1))
            e7 = UNIT * ((u7 - up7) + (v7 - jnp.where(lane == 0, 0.0, lroll(v7, 1))))
            e0 = UNIT * ((u0 - up0) + (v0 - jnp.where(lane == 0, 0.0, lroll(v0, 1))))
            ea = jnp.where(sub < 2, sroll(e7, -3), pb[z, top:, :])
            eb = jnp.where(sub < 3, sroll(e7, -5), w[z, top:, :])
            wa = jnp.where(sub < 6, pb[z, 0:SUBL, :], sroll(e0, 6))
            wb = jnp.where(sub < 5, w[z, 0:SUBL, :], sroll(e0, 3))
            at = 2 * SUBL * c5
            xa[h, at : at + SUBL, :] = jnp.where(even, ea, wa)
            xa[h, at + SUBL : at + 2 * SUBL, :] = jnp.where(even, eb, wb)
            xb[h, at : at + SUBL, :] = jnp.where(even, wa, ea)
            xb[h, at + SUBL : at + 2 * SUBL, :] = jnp.where(even, wb, eb)
            last = ub[z, size_x - 1 : size_x, :]
            xa[h, 80 + c5 : 81 + c5, :] = last
            xb[h, 80 + c5 : 81 + c5, :] = last
        for f in range(4):
            c_out[0, f * (ZC // 5) + h] = corners[f]
        return carry

    lax.fori_loop(0, ZC // 5, body, 0)
    strip = strip_of(lambda b: r[SUBL * b : SUBL * (b + 1), :])
    q[0, 4 * ZC] = strip
    c_out[0, 4 * (ZC // 5)] = corner_of(strip, 0, jnp.zeros((SUBL, LANES), F32))
    east_r = r[size_x - 5 : size_x, :]
    west_r = r[0:5, :]
    ra = jnp.where(even, east_r, west_r)
    rb = jnp.where(even, west_r, east_r)
    for ref, val in ((xa, ra), (xb, rb)):
        ref[0, 85:88, :] = val[0:3]
        ref[1, 85:87, :] = val[3:5]
        ref[1, 87:88, :] = val[4:5]
        ref[2, 85:88, :] = val[0:3]
        ref[3, 85:88, :] = val[0:3]


def substeps(n_gx, n_gy, *refs):
    (ub, vb, pb, w, r, xa, xb, qa, qb, ca, cb, caa, cab, cba, cbb) = refs[:15]
    (u_out, v_out, w_out, p_out) = refs[15:19]
    (PM, PS, FM, WM, GM, QM, LM, SM, KM) = refs[19:]
    levels, size_x = ub.shape[0], ub.shape[1]
    blocks = size_x // SUBL
    full = blocks + 2
    every = range(full + 1)
    gx = lax.axis_index("gx")
    gy = lax.axis_index("gy")
    x_even = (gx % 2) == 0
    y_even = (gy % 2) == 0
    is_w, is_e = gx == 0, gx == n_gx - 1
    is_s, is_n = gy == 0, gy == n_gy - 1
    lane = lane_ids()
    sub = sub_ids()
    within = lane % GROUP
    block_of = lane // GROUP
    low_half = within < DEEP
    rim_lo, rim_hi = within == DEEP - 1, within == DEEP
    zero = jnp.zeros((SUBL, LANES), F32)
    rows = [slice(SUBL * b, SUBL * (b + 1)) for b in range(full + 2)]
    COEF, RINV, STEP = 0, 1, 2

    def strip_from(mine, cw, ce, spot):
        o = 2 * GROUP * spot
        got = jnp.where(block_of == 0, lroll(cw, -o), mine)
        return jnp.where(block_of == full - 1, lroll(ce, GROUP * blocks - o), got)

    def four(k, i):
        aa, ab, ba, bb = caa[k, i], cab[k, i], cba[k, i], cbb[k, i]
        a_s, a_n = jnp.where(y_even, ab, aa), jnp.where(y_even, aa, ab)
        b_s, b_n = jnp.where(y_even, bb, ba), jnp.where(y_even, ba, bb)
        a, b = jnp.where(low_half, a_s, a_n), jnp.where(low_half, b_s, b_n)
        return jnp.where(x_even, b, a), jnp.where(x_even, a, b)

    def strip_at(k, iq, corners, spot):
        a, b = qa[k, iq], qb[k, iq]
        mine = jnp.where(low_half == y_even, b, a)
        return strip_from(mine, corners[0], corners[1], spot)

    def strip_rows(s):
        up = sroll(s, 1)
        up = jnp.where(sub == 0, lroll(up, GROUP), up)
        dn = sroll(s, -1)
        dn = jnp.where(sub == SUBL - 1, lroll(dn, -GROUP), dn)
        return up, dn

    row_first = is_w & (block_of == 1) & (sub == 0)
    row_last = is_e & (block_of == full - 2) & (sub == SUBL - 1)
    lane0, lane_end = lane == 0, lane == LANES - 1
    lane0_in, lane0_rim = lane0 & jnp.logical_not(is_s), lane0 & is_s
    strip_zero = is_n & rim_hi
    fix_w, fix_e = is_w & (sub == SUBL - 1), is_e & (sub == 0)

    def put_pressure(z, tiles):
        tiles = list(tiles)
        tiles[0] = jnp.where(fix_w, sroll(tiles[1], -1), tiles[0])
        tiles[full - 1] = jnp.where(fix_e, 0.0, tiles[full - 1])
        ps = jnp.where(strip_zero, 0.0, tiles[full])
        PS[z] = ps
        s_lf, s_rt = lroll(ps, 1), lroll(ps, -1)
        for b in range(full):
            p0 = tiles[b]
            PM[z, rows[b + 1], :] = p0
            lo = GROUP * b + DEEP
            s_lf = jnp.where(lane == lo, lroll(p0, lo + 1), s_lf)
            s_rt = jnp.where(lane == lo - 1, lroll(p0, lo - 1), s_rt)
            lf = jnp.where(lane0_in, lroll(ps, 1 - lo), lroll(p0, 1))
            lf = jnp.where(lane0_rim, p0, lf)
            rt = jnp.where(lane_end, lroll(ps, -1 - lo), lroll(p0, -1))
            LM[z, rows[b], :] = lf + rt
        up, dn = strip_rows(ps)
        up = jnp.where(row_first, ps, up)
        dn = jnp.where(row_last, 0.0, dn)
        LM[z, rows[full], :] = (s_lf + s_rt) + (up + dn)

    west_x = lambda h, lo, hi: jnp.where(x_even, xb[h, lo:hi, :], xa[h, lo:hi, :])
    east_x = lambda h, lo, hi: jnp.where(x_even, xa[h, lo:hi, :], xb[h, lo:hi, :])
    KM[COEF] = jnp.ones((SUBL * (full + 1), LANES), F32)
    KM[COEF, SUBL : SUBL * (blocks + 1), :] = r[...]
    KM[COEF, 3:6, :] = west_x(0, 85, 88)
    KM[COEF, 6:8, :] = west_x(1, 85, 87)
    lo = SUBL * (full - 1)
    KM[COEF, lo : lo + 3, :] = east_x(0, 85, 88)
    KM[COEF, lo + 3 : lo + 5, :] = east_x(1, 85, 87)
    KM[COEF, rows[full], :] = strip_at(0, 4 * ZC, four(0, 4 * (ZC // 5)), 0)
    kappas, rhos = [], []
    for b in every:
        c = KM[COEF, rows[b], :]
        c = jnp.where(c > 0.0, c, 1.0)
        KM[COEF, rows[b], :] = c
        KM[RINV, rows[b], :] = 1.0 / c
        KM[STEP, rows[b], :] = BUOYANCY / c
        k = 2.0 * c / ((1.0 + 2.0 * c) + jnp.sqrt(1.0 + 4.0 * c))
        kappas.append(k)
        rhos.append(k * k)

    def factor_body(z, carry):
        powers, lows = carry
        new_p, new_l = [], []
        for b in every:
            nxt = powers[b] * rhos[b]
            high = 1.0 - nxt
            GM[z + 1, rows[b], :] = kappas[b] * (lows[b] / high)
            new_p.append(nxt)
            new_l.append(high)
        return tuple(new_p), tuple(new_l)

    lax.fori_loop(0, levels, factor_body, (tuple(rhos), tuple(1.0 - x for x in rhos)))
    wide = jnp.zeros((SUBL * (full + 1), LANES), F32)
    GM[0] = wide
    WM[0] = wide
    QM[levels] = wide
    FM[levels] = wide
    LM[levels] = wide
    PM[levels] = jnp.zeros((SUBL * (full + 2), LANES), F32)
    PS[levels] = zero
    SM[levels] = jnp.zeros((SUBL * (blocks + 2), LANES), F32)

    s5 = ZC // 5

    def unpack(h, carry):
        k, hh = h // s5, h % s5
        corners = [four(k, f * s5 + hh) for f in range(4)]
        i_v = s5 + hh
        v_w = jnp.where(x_even, cb[k, i_v], ca[k, i_v])
        v_e = jnp.where(x_even, ca[k, i_v], cb[k, i_v])
        for c5 in range(5):
            z, zz = h * 5 + c5, hh * 5 + c5
            us, vs, ps, ws = [strip_at(k, f * ZC + zz, corners[f], c5) for f in range(4)]
            at = 2 * SUBL * c5
            xa_a, xa_b = xa[h, at : at + SUBL, :], xa[h, at + SUBL : at + 2 * SUBL, :]
            xb_a, xb_b = xb[h, at : at + SUBL, :], xb[h, at + SUBL : at + 2 * SUBL, :]
            wa, wb = jnp.where(x_even, xb_a, xa_a), jnp.where(x_even, xb_b, xa_b)
            ea, eb = jnp.where(x_even, xa_a, xb_a), jnp.where(x_even, xa_b, xb_b)
            f_west = jnp.where(sub < 5, sroll(wa, 3), sroll(wb, 5))
            f_east = jnp.where(sub < 2, sroll(ea, 2), sroll(eb, -3))
            u_row = jnp.where(x_even, xb[h, 80 + c5 : 81 + c5, :], xa[h, 80 + c5 : 81 + c5, :])
            u_row = jnp.where(is_w, 0.0, u_row)
            vm = [vb[z, rows[b], :] for b in range(blocks)]
            v_left = jnp.where(rim_hi, zero, lroll(vs, 1))
            far = strip_from(zero, v_w, v_e, c5)
            v_left = jnp.where(rim_hi, lroll(far, 1), v_left)
            for b in range(blocks):
                lo = GROUP * (b + 1) + DEEP
                v_left = jnp.where(lane == lo, lroll(vm[b], lo + 1), v_left)
            u_up, _ = strip_rows(us)
            FM[z, rows[full], :] = UNIT * ((us - u_up) + (vs - v_left))
            WM[z + 1, rows[full], :] = ws * KM[RINV, rows[full], :]
            tiles = [wa] + [pb[z, rows[b], :] for b in range(blocks)] + [ea, ps]
            put_pressure(z, tiles)
            for b in range(full):
                v_rim = jnp.where(lane0, lroll(vs, 1 - (GROUP * b + DEEP)), 0.0)
                if b == 0:
                    e, ww = f_west - UNIT * v_rim, wb
                elif b == full - 1:
                    u63 = jnp.where(sub == 0, sroll(ub[z, rows[blocks - 1], :], 1), 0.0)
                    e, ww = f_east - UNIT * (v_rim + u63), eb
                else:
                    m = b - 1
                    uu = ub[z, rows[m], :]
                    if m == 0:
                        up = jnp.where(sub == 0, u_row, sroll(uu, 1))
                    else:
                        up = ub[z, SUBL * m - 1 : SUBL * (m + 1) - 1, :]
                    left = jnp.where(lane0, v_rim, lroll(vm[m], 1))
                    e = UNIT * ((uu - up) + (vm[m] - left))
                    ww = w[z, rows[m], :]
                FM[z, rows[b], :] = e
                WM[z + 1, rows[b], :] = ww * KM[RINV, rows[b], :]
            SM[z] = jnp.zeros((SUBL * (blocks + 2), LANES), F32)
            PM[z, rows[0], :] = zero
            PM[z, rows[full + 1], :] = zero
        return carry

    lax.fori_loop(0, levels // 5, unpack, 0)

    coef_step = ACCEL * SPREAD
    inner = range(1, full - 1)

    def section(z, last):
        qs = {}
        for b in every:
            p0 = PM[z, rows[b + 1], :] if b < full else PS[z]
            if b >= 1:
                SM[z, rows[b - 1], :] += p0
            if last and b not in inner:
                continue
            around = LM[z, rows[b], :]
            if b < full:
                up = PM[z, SUBL * (b + 1) - 1 : SUBL * (b + 2) - 1, :]
                dn = PM[z, SUBL * (b + 1) + 1 : SUBL * (b + 2) + 1, :]
                around = around + (up + dn)
            f = FM[z, rows[b], :] + (4.0 * p0 - around)
            if not last:
                FM[z, rows[b], :] = f
            qq = p0 - coef_step * f
            QM[z, rows[b], :] = qq
            qs[b] = qq
        return qs

    def run_step(last):
        active = inner if last else every

        def forward(i, carry):
            q_here = dict(zip(active, carry[0]))
            d_prev = dict(zip(active, carry[1]))
            for z in (2 * i, 2 * i + 1):
                q_next = section(z + 1, last)
                for b in active:
                    rhs = WM[z + 1, rows[b], :] + KM[STEP, rows[b], :] * (q_here[b] - q_next[b])
                    d = GM[z + 1, rows[b], :] * (rhs + d_prev[b])
                    WM[z + 1, rows[b], :] = d
                    d_prev[b] = d
                q_here = q_next
            return tuple(q_here[b] for b in active), tuple(d_prev[b] for b in active)

        q0 = section(0, last)
        start = (tuple(q0[b] for b in active), tuple(zero for _ in active))
        _, tops = lax.fori_loop(0, levels // 2, forward, start)
        if not last:
            for b, top in zip(active, tops):
                WM[levels, rows[b], :] = top * KM[RINV, rows[b], :]

        def backward(i, above):
            above = dict(zip(active, above))
            for c in range(4):
                z = levels - 1 - (4 * i + c)
                tiles = {}
                below = {}
                for b in active:
                    ww = WM[z, rows[b], :] + GM[z, rows[b], :] * above[b]
                    tiles[b] = QM[z, rows[b], :] - BUOYANCY * (above[b] - ww)
                    if not last:
                        WM[z, rows[b], :] = ww * KM[RINV, rows[b], :]
                    below[b] = ww
                if last:
                    ss = SM[z, rows[blocks + 1], :]
                    for b in active:
                        m = rows[b - 1]
                        w_out[z, m, :] = above[b]
                        p_out[z, m, :] = tiles[b]
                        s0 = SM[z, m, :]
                        dn = SM[z, SUBL * (b - 1) + 1 : SUBL * b + 1, :]
                        rt = jnp.where(
                            lane_end, lroll(ss, -1 - (GROUP * b + DEEP)), lroll(s0, -1)
                        )
                        u_out[z, m, :] = ub[z, m, :] - ACCEL * (dn - s0)
                        v_out[z, m, :] = vb[z, m, :] - ACCEL * (rt - s0)
                else:
                    put_pressure(z, [tiles[b] for b in every])
                above = below
            return tuple(above[b] for b in active)

        lax.fori_loop(0, levels // 4, backward, tops)

    def step(_, carry):
        run_step(False)
        return carry

    lax.fori_loop(0, SUBSTEPS - 1, step, 0)
    run_step(True)


def swap(block, axis, second):
    n = lax.axis_size(axis)
    return lax.ppermute(block, axis, pairing(n, second))


def pairing(n, second):
    lo = 1 if second else 0
    pairs = []
    for i in range(lo, n - 1, 2):
        pairs += [(i, i + 1), (i + 1, i)]
    return pairs


def swap2(block, second_x, second_y):
    nx, ny = lax.axis_size("gx"), lax.axis_size("gy")
    pairs = []
    for a, b in pairing(nx, second_x):
        for c, d in pairing(ny, second_y):
            pairs.append((a * ny + c, b * ny + d))
    return lax.ppermute(block, ("gx", "gy"), pairs)


def to_ends(low, high, axis):
    n = lax.axis_size(axis)
    me = lax.axis_index(axis)
    got = []
    for k in range(1, n):
        block = jnp.where(me == k, low, high)
        got.append(lax.ppermute(block, axis, [(k, 0), (n - 1 - k, n - 1)]))
    return got


def per_device(u_wind, v_wind, w_wind, pressure, vert_coef, we_slab, sn_slab, relax_width):
    n_gx, n_gy = lax.axis_size("gx"), lax.axis_size("gy")
    levels, size_x, size_y = pressure.shape
    blocks = size_x // SUBL
    full = blocks + 2
    band, m = we_slab.shape[3], we_slab.shape[4]
    xs = sn_slab.shape[4]
    steps = levels // ZC
    sds = jax.ShapeDtypeStruct
    big = pltpu.CompilerParams(vmem_limit_bytes=60 * 1024 * 1024)

    sn_t = jnp.transpose(sn_slab, (0, 1, 2, 4, 3))
    we_shape = (steps, 3, ZC // 4, SUBL, LANES)
    sn_shape = (steps, 3, ZC // 10, SUBL, LANES)
    lead = lambda shape: pl.BlockSpec((1,) + shape[1:], lambda i: (i,) + (0,) * (len(shape) - 1))
    west, east, south, north = pl.pallas_call(
        pack_slabs,
        grid=(steps,),
        in_specs=[
            pl.BlockSpec((2, 3, ZC, band, m), lambda i: (0, 0, i, 0, 0)),
            pl.BlockSpec((2, 3, ZC, xs, band), lambda i: (0, 0, i, 0, 0)),
        ],
        out_specs=[lead(we_shape)] * 2 + [lead(sn_shape)] * 2,
        out_shape=[sds(we_shape, F32)] * 2 + [sds(sn_shape, F32)] * 2,
        name="pack_slabs",
    )(we_slab, sn_t)
    we_in = to_ends(west, east, "gx")
    sn_in = to_ends(south, north, "gy")

    field = pl.BlockSpec((ZC, size_x, size_y), lambda i: (i, 0, 0))
    plane = pl.BlockSpec((size_x, size_y), lambda i: (0, 0))
    x_shape = (levels // 5, 88, LANES)
    q_shape = (steps, 4 * ZC + 1, SUBL, LANES)
    c_shape = (steps, 4 * (ZC // 5) + 1, SUBL, LANES)
    ub, vb, pb, xa, xb, q, c = pl.pallas_call(
        functools.partial(blend_pack, n_gx, n_gy, m, xs, band),
        grid=(steps,),
        in_specs=[field] * 4
        + [plane] * 2
        + [lead(we_shape)] * 2
        + [lead(sn_shape)] * 2
        + [lead(we_shape)] * (n_gx - 1)
        + [lead(sn_shape)] * (n_gy - 1),
        out_specs=[field] * 3
        + [pl.BlockSpec((ZC // 5, 88, LANES), lambda i: (i, 0, 0))] * 2
        + [lead(q_shape), lead(c_shape)],
        out_shape=[sds(pressure.shape, F32)] * 3
        + [sds(x_shape, F32)] * 2
        + [sds(q_shape, F32), sds(c_shape, F32)],
        compiler_params=big,
        name="blend_pack",
    )(
        u_wind, v_wind, pressure, w_wind, vert_coef, relax_width,
        west, east, south, north, *we_in, *sn_in,
    )
    xa = swap(xa, "gx", False)
    xb = swap(xb, "gx", True)
    qa = swap(q, "gy", False)
    qb = swap(q, "gy", True)
    ca = swap(c, "gx", False)
    cb = swap(c, "gx", True)
    caa = swap2(c, False, False)
    cab = swap2(c, False, True)
    cba = swap2(c, True, False)
    cbb = swap2(c, True, True)

    whole = pl.BlockSpec(memory_space=pltpu.VMEM)
    tall = pltpu.VMEM((levels + 1, SUBL * (full + 1), LANES), F32)
    return pl.pallas_call(
        functools.partial(substeps, n_gx, n_gy),
        in_specs=[whole] * 15,
        out_specs=[whole] * 4,
        out_shape=[sds(pressure.shape, F32)] * 4,
        scratch_shapes=[
            pltpu.VMEM((levels + 1, SUBL * (full + 2), LANES), F32),
            pltpu.VMEM((levels + 1, SUBL, LANES), F32),
            tall, tall, tall, tall, tall,
            pltpu.VMEM((levels + 1, SUBL * (blocks + 2), LANES), F32),
            pltpu.VMEM((3, SUBL * (full + 1), LANES), F32),
        ],
        compiler_params=big,
        name="substeps",
    )(ub, vb, pb, w_wind, vert_coef, xa, xb, qa, qb, ca, cb, caa, cab, cba, cbb)


def solution(mesh):
    cell = P(None, "gx", "gy")
    placed = (
        cell, cell, cell, cell,
        P("gx", "gy"),
        P(None, None, None, None, ("gy", "gx")),
        P(None, None, None, None, ("gx", "gy")),
        P("gx", "gy"),
    )
    return jax.shard_map(
        per_device,
        mesh=mesh,
        in_specs=placed,
        out_specs=(cell, cell, cell, cell),
        check_vma=False,
    )
```

time: 297 us -> 182 us (0.61)
  Pallas kernels: 192 us -> 79.5 us
  starting transfers between devices: 49.6 us -> 45.1 us
    pallas_call x1, Pallas kernels: 174 us -> 61.6 us  [per_device(): pl.pallas_call(functools.partial(substeps, n_gx, n_gy), in_specs=[whole]...]
    ppermute x4, starting transfers between devices: 14.7 us -> 10.2 us  [swap2(): return lax.ppermute(block, ('gx', 'gy'), pairs)]
  transfers between devices with their start and end apart: 20 -> 20, of which waited for: 5 -> 5; matrix products, arithmetic and copies ran while one was open for 0% -> 1% of each run, Pallas kernels for 0% -> 0%
where the time goes in v1:
time: 182 us
  Pallas kernels  79.5 us (44%)
  waiting for transfers between devices  46.4 us (25%)
  starting transfers between devices  45.1 us (25%)
  local copies, waits for them, and re-layouts  7.55 us (4%)
  other arithmetic  2.01 us (1%)
    pallas_call x1, Pallas kernels, per_device(): pl.pallas_call(functools.partial(substeps, n_gx, n_gy), in_specs=[whole]...  61.6 us
    ppermute x6, waiting for transfers between devices, swap(): return lax.ppermute(block, axis, pairing(n, second))  31.8 us
    ppermute x10, starting transfers between devices, to_ends(): got.append(lax.ppermute(block, axis, [(k, 0), (n - 1 - k, n - 1)]))  25.8 us
    pallas_call x1, Pallas kernels, per_device(): pl.pallas_call(functools.partial(blend_pack, n_gx, n_gy, m, xs, band), gr...  13.7 us
    ppermute x4, waiting for transfers between devices, swap2(): return lax.ppermute(block, ('gx', 'gy'), pairs)  13.3 us
    ppermute x4, starting transfers between devices, swap2(): return lax.ppermute(block, ('gx', 'gy'), pairs)  10.2 us
    ppermute x6, starting transfers between devices, swap(): return lax.ppermute(block, axis, pairing(n, second))  9.06 us
    unnamed x44, local copies, waits for them, and re-layouts  7.55 us
  transfers between devices with their start and end apart: 20, of which 5 were waited for; matrix products, arithmetic and copies ran while one was open for 1% of the time, Pallas kernels for 0%

profile of v1, /device:TPU:10, one launch (start us, length us, event | category | flops | bytes accessed | tf_op | source)
XLA Modules:
  0.0 181.7 jit_solution(7615635453817174410)
XLA Ops:
  0.7 2.7 %copy.13.we = f32[2,3,60,5,32]{4,3,2,1,0:T(8,128)} copy(f32[2,3,60,5,32]{2,4,3,1,0:T(8,128)} %param.13) | data formatting | bytes 460800 | tf_op args[5]
  3.4 1.7 copy.12
  5.1 4.2 %pack_slabs.1 = (f32[3,3,5,8,128]{4,3,2,1,0:T(8,128)}, f32[3,3,5,8,128]{4,3,2,1,0:T(8,128)}, f32[3,3,2,8,128]{4,3,2,1,0:T(8,128)}, f32[3,3,2,8,128]{4,3,2,1,0:T(8,128)}) custom-call(f32[2,3,60,5,32]{4,3,2,1,0:T(8,128)} %copy.13.we, f32[2,3,60,8,5]{4,3,2,1,0:T(8,128)} %bitcast.1), custom_call_target="tpu_custom_call" | custom-call | tf_op jit(solution)/shard_map/pack_slabs/pallas_call | solution.py:540
  9.3 1.0 broadcast_select_fusion.3
  10.3 0.7 collective-permute-start.9
  11.0 0.7 collective-permute-start.8
  11.6 6.3 %collective-permute-start.7 = (f32[3,3,2,8,128]{4,3,2,1,0:T(8,128)S(1)}, f32[3,3,2,8,128]{4,3,2,1,0:T(8,128)S(1)}, u32[]{:S(2)}, u32[]{:S(2)}) collective-permute-start(f32[3,3,2,8,128]{4,3,2,1,0:T(8,128)S(1)} %get-tuple-element.31), channel_id=1, source_target_pairs={{5,0},{2,7},{13,8},{10,15},{21,16},{18,23},{29,24},{26,31}} | collective-permute-start | bytes 221192 | tf_op jit(solution)/shard_map/ppermute | solution.py:521
  18.0 1.1 broadcast_select_fusion
  19.0 0.7 collective-permute-start.2
  19.7 4.7 %collective-permute-start.1 = (f32[3,3,5,8,128]{4,3,2,1,0:T(8,128)S(1)}, f32[3,3,5,8,128]{4,3,2,1,0:T(8,128)S(1)}, u32[]{:S(2)}, u32[]{:S(2)}) collective-permute-start(f32[3,3,5,8,128]{4,3,2,1,0:T(8,128)S(1)} %get-tuple-element.27), channel_id=1, source_target_pairs={{16,0},{8,24},{17,1},{9,25},{18,2},{10,26},{19,3},{11,27},{20,4},{... | collective-permute-start | bytes 552968 | tf_op jit(solution)/shard_map/ppermute | solution.py:521
  24.4 2.7 %collective-permute-start = (f32[3,3,5,8,128]{4,3,2,1,0:T(8,128)S(1)}, f32[3,3,5,8,128]{4,3,2,1,0:T(8,128)S(1)}, u32[]{:S(2)}, u32[]{:S(2)}) collective-permute-start(f32[3,3,5,8,128]{4,3,2,1,0:T(8,128)S(1)} %get-tuple-element.28), channel_id=1, source_target_pairs={{8,0},{16,24},{9,1},{17,25},{10,2},{18,26},{11,3},{19,27},{12,4},{... | collective-permute-start | bytes 552968 | tf_op jit(solution)/shard_map/ppermute | solution.py:521
  27.2 0.7 collective-permute-start.6
  27.9 0.7 collective-permute-start.5
  28.6 8.1 %collective-permute-start.4 = (f32[3,3,2,8,128]{4,3,2,1,0:T(8,128)S(1)}, f32[3,3,2,8,128]{4,3,2,1,0:T(8,128)S(1)}, u32[]{:S(2)}, u32[]{:S(2)}) collective-permute-start(f32[3,3,2,8,128]{4,3,2,1,0:T(8,128)S(1)} %get-tuple-element.34), channel_id=1, source_target_pairs={{2,0},{5,7},{10,8},{13,15},{18,16},{21,23},{26,24},{29,31}} | collective-permute-start | bytes 221192 | tf_op jit(solution)/shard_map/ppermute | solution.py:521
  36.7 0.7 collective-permute-start.3
  37.4 1.3 collective-permute-done.4.refs_14_
  38.7 0.5 copy-done.19
  39.4 0.7 copy-done.12
  40.1 13.7 %blend_pack.1 = (f32[60,64,128]{2,1,0:T(8,128)}, f32[60,64,128]{2,1,0:T(8,128)}, f32[60,64,128]{2,1,0:T(8,128)}, f32[12,88,128]{2,1,0:T(8,128)}, f32[12,88,128]{...) custom-call(f32[60,64,128]{2,1,0:T(8,128)} %refs_0_.1, f32[60,64,128]{2,1,0:T(8,128)} %refs_1_.1, ...), custom_call_target="tpu_custom_call" | custom-call | tf_op jit(solution)/shard_map/blend_pack/pallas_call | solution.py:559
  53.8 2.2 %collective-permute-start.13 = (f32[3,81,8,128]{3,2,1,0:T(8,128)}, f32[3,81,8,128]{3,2,1,0:T(8,128)S(1)}, u32[]{:S(2)}, u32[]{:S(2)}) collective-permute-start(f32[3,81,8,128]{3,2,1,0:T(8,128)} %get-tuple-element.24), channel_id=1, source_target_pairs={{1,2},{2,1},{3,4},{4,3},{5,6},{6,5},{9,10},{10,9},{11,12},{12,11},... | collective-permute-start | bytes 2985992 | tf_op jit(solution)/shard_map/ppermute | solution.py:495
  56.2 6.3 %collective-permute-start.19 = (f32[3,17,8,128]{3,2,1,0:T(8,128)}, f32[3,17,8,128]{3,2,1,0:T(8,128)S(1)}, u32[]{:S(2)}, u32[]{:S(2)}) collective-permute-start(f32[3,17,8,128]{3,2,1,0:T(8,128)} %get-tuple-element.25), channel_id=1, source_target_pairs={{9,18},{10,17},{11,20},{12,19},{13,22},{14,21},{17,10},{18,9},{19,... | collective-permute-start | bytes 626696 | tf_op jit(solution)/shard_map/ppermute | solution.py:512
  62.5 1.9 %collective-permute-start.18 = (f32[3,17,8,128]{3,2,1,0:T(8,128)}, f32[3,17,8,128]{3,2,1,0:T(8,128)S(1)}, u32[]{:S(2)}, u32[]{:S(2)}) collective-permute-start(f32[3,17,8,128]{3,2,1,0:T(8,128)} %get-tuple-element.25), channel_id=1, source_target_pairs={{8,17},{9,16},{10,19},{11,18},{12,21},{13,20},{14,23},{15,22},{16,... | collective-permute-start | bytes 626696 | tf_op jit(solution)/shard_map/ppermute | solution.py:512
  64.4 1.9 %collective-permute-start.17 = (f32[3,17,8,128]{3,2,1,0:T(8,128)}, f32[3,17,8,128]{3,2,1,0:T(8,128)S(1)}, u32[]{:S(2)}, u32[]{:S(2)}) collective-permute-start(f32[3,17,8,128]{3,2,1,0:T(8,128)} %get-tuple-element.25), channel_id=1, source_target_pairs={{1,10},{2,9},{3,12},{4,11},{5,14},{6,13},{9,2},{10,1},{11,4},{12,3... | collective-permute-start | bytes 626696 | tf_op jit(solution)/shard_map/ppermute | solution.py:512
  66.4 6.8 %collective-permute-done.19.refs_14_ = f32[3,17,8,128]{3,2,1,0:T(8,128)S(1)} collective-permute-done((f32[3,17,8,128]{3,2,1,0:T(8,128)}, f32[3,17,8,128]{3,2,1,0:T(8,128)S(1)}, u32[]{:S(2)}, u32[]{:S(2)}) %collective-permute-start.19) | collective-permute-done | bytes 208928 | tf_op jit(solution)/shard_map/ppermute | solution.py:512
  73.1 6.6 %collective-permute-done.18.refs_13_ = f32[3,17,8,128]{3,2,1,0:T(8,128)S(1)} collective-permute-done((f32[3,17,8,128]{3,2,1,0:T(8,128)}, f32[3,17,8,128]{3,2,1,0:T(8,128)S(1)}, u32[]{:S(2)}, u32[]{:S(2)}) %collective-permute-start.18) | collective-permute-done | bytes 208928 | tf_op jit(solution)/shard_map/ppermute | solution.py:512
  79.7 3.4 %collective-permute-start.11 = (f32[12,88,128]{2,1,0:T(8,128)}, f32[12,88,128]{2,1,0:T(8,128)S(1)}, u32[]{:S(2)}, u32[]{:S(2)}) collective-permute-start(f32[12,88,128]{2,1,0:T(8,128)} %get-tuple-element.23), channel_id=1, source_target_pairs={{8,16},{16,8},{9,17},{17,9},{10,18},{18,10},{11,19},{19,11},{12,20... | collective-permute-start | bytes 1622024 | tf_op jit(solution)/shard_map/ppermute | solution.py:495
  83.1 3.4 %collective-permute-start.15 = (f32[3,17,8,128]{3,2,1,0:T(8,128)}, f32[3,17,8,128]{3,2,1,0:T(8,128)S(1)}, u32[]{:S(2)}, u32[]{:S(2)}) collective-permute-start(f32[3,17,8,128]{3,2,1,0:T(8,128)} %get-tuple-element.25), channel_id=1, source_target_pairs={{8,16},{16,8},{9,17},{17,9},{10,18},{18,10},{11,19},{19,11},{12,20... | collective-permute-start | bytes 626696 | tf_op jit(solution)/shard_map/ppermute | solution.py:495
  86.5 24.1 %collective-permute-done.15.refs_10_ = f32[3,17,8,128]{3,2,1,0:T(8,128)S(1)} collective-permute-done((f32[3,17,8,128]{3,2,1,0:T(8,128)}, f32[3,17,8,128]{3,2,1,0:T(8,128)S(1)}, u32[]{:S(2)}, u32[]{:S(2)}) %collective-permute-start.15) | collective-permute-done | bytes 208928 | tf_op jit(solution)/shard_map/ppermute | solution.py:495
  110.6 7.7 %collective-permute-done.14.refs_9_ = f32[3,17,8,128]{3,2,1,0:T(8,128)S(1)} collective-permute-done((f32[3,17,8,128]{3,2,1,0:T(8,128)}, f32[3,17,8,128]{3,2,1,0:T(8,128)S(1)}, u32[]{:S(2)}, u32[]{:S(2)}) %collective-permute-start.14) | collective-permute-done | bytes 208928 | tf_op jit(solution)/shard_map/ppermute | solution.py:495
  118.4 0.6 copy-done.9
  119.7 0.3 copy-done.1
  120.1 61.6 %substeps.1 = (f32[60,64,128]{2,1,0:T(8,128)}, f32[60,64,128]{2,1,0:T(8,128)}, f32[60,64,128]{2,1,0:T(8,128)}, f32[60,64,128]{2,1,0:T(8,128)}) custom-call(f32[60,64,128]{2,1,0:T(8,128)} %get-tuple-element.19.refs_0_, f32[60,64,128]{2,1,0:T(8,128)} %get-tuple-element.20.refs_1_, f32[60,64,128]{2,1,0:T(8,128)} %get-tuple-element.21.refs_2_, ...), custom_call_target="tpu_custom_call" | custom-call | tf_op jit(solution)/shard_map/substeps/pallas_call | solution.py:593
  (57 shorter events, 1.0 us)
Async XLA Ops:
  0.6 2.8 %copy-start.13 = (f32[2,3,60,5,8]{2,4,3,1,0:T(8,128)S(1)}, f32[2,3,60,5,8]{2,4,3,1,0:T(8,128)}, u32[]{:S(2)}) copy-start(f32[2,3,60,5,8]{2,4,3,1,0:T(8,128)} %param.14) | copy-start | bytes 172804
  10.3 14.1 %collective-permute-start.9 = (f32[3,3,2,8,128]{4,3,2,1,0:T(8,128)S(1)}, f32[3,3,2,8,128]{4,3,2,1,0:T(8,128)S(1)}, u32[]{:S(2)}, u32[]{:S(2)}) collective-permute-start(f32[3,3,2,8,128]{4,3,2,1,0:T(8,128)S(1)} %get-tuple-element.29), channel_id=1, source_target_pairs={{7,0},{0,7},{15,8},{8,15},{23,16},{16,23},{31,24},{24,31}} | collective-permute-start | bytes 221192 | tf_op jit(solution)/shard_map/ppermute | solution.py:521
  11.0 16.2 %collective-permute-start.8 = (f32[3,3,2,8,128]{4,3,2,1,0:T(8,128)S(1)}, f32[3,3,2,8,128]{4,3,2,1,0:T(8,128)S(1)}, u32[]{:S(2)}, u32[]{:S(2)}) collective-permute-start(f32[3,3,2,8,128]{4,3,2,1,0:T(8,128)S(1)} %get-tuple-element.30), channel_id=1, source_target_pairs={{6,0},{1,7},{14,8},{9,15},{22,16},{17,23},{30,24},{25,31}} | collective-permute-start | bytes 221192 | tf_op jit(solution)/shard_map/ppermute | solution.py:521
  11.6 16.2 %collective-permute-start.7 = (f32[3,3,2,8,128]{4,3,2,1,0:T(8,128)S(1)}, f32[3,3,2,8,128]{4,3,2,1,0:T(8,128)S(1)}, u32[]{:S(2)}, u32[]{:S(2)}) collective-permute-start(f32[3,3,2,8,128]{4,3,2,1,0:T(8,128)S(1)} %get-tuple-element.31), channel_id=1, source_target_pairs={{5,0},{2,7},{13,8},{10,15},{21,16},{18,23},{29,24},{26,31}} | collective-permute-start | bytes 221192 | tf_op jit(solution)/shard_map/ppermute | solution.py:521
  19.0 19.6 %collective-permute-start.2 = (f32[3,3,5,8,128]{4,3,2,1,0:T(8,128)S(1)}, f32[3,3,5,8,128]{4,3,2,1,0:T(8,128)S(1)}, u32[]{:S(2)}, u32[]{:S(2)}) collective-permute-start(f32[3,3,5,8,128]{4,3,2,1,0:T(8,128)S(1)} %get-tuple-element.26), channel_id=1, source_target_pairs={{24,0},{0,24},{25,1},{1,25},{26,2},{2,26},{27,3},{3,27},{28,4},{4,... | collective-permute-start | bytes 552968 | tf_op jit(solution)/shard_map/ppermute | solution.py:521
  19.7 19.0 %collective-permute-start.1 = (f32[3,3,5,8,128]{4,3,2,1,0:T(8,128)S(1)}, f32[3,3,5,8,128]{4,3,2,1,0:T(8,128)S(1)}, u32[]{:S(2)}, u32[]{:S(2)}) collective-permute-start(f32[3,3,5,8,128]{4,3,2,1,0:T(8,128)S(1)} %get-tuple-element.27), channel_id=1, source_target_pairs={{16,0},{8,24},{17,1},{9,25},{18,2},{10,26},{19,3},{11,27},{20,4},{... | collective-permute-start | bytes 552968 | tf_op jit(solution)/shard_map/ppermute | solution.py:521
  24.4 14.3 %copy-start.14 = (f32[3,3,2,8,128]{4,3,2,1,0:T(8,128)}, f32[3,3,2,8,128]{4,3,2,1,0:T(8,128)S(1)}, u32[]{:S(2)}) copy-start(f32[3,3,2,8,128]{4,3,2,1,0:T(8,128)S(1)} %collective-permute-done.9.refs_19_) | copy-start | bytes 221188
  24.4 14.3 %collective-permute-start = (f32[3,3,5,8,128]{4,3,2,1,0:T(8,128)S(1)}, f32[3,3,5,8,128]{4,3,2,1,0:T(8,128)S(1)}, u32[]{:S(2)}, u32[]{:S(2)}) collective-permute-start(f32[3,3,5,8,128]{4,3,2,1,0:T(8,128)S(1)} %get-tuple-element.28), channel_id=1, source_target_pairs={{8,0},{16,24},{9,1},{17,25},{10,2},{18,26},{11,3},{19,27},{12,4},{... | collective-permute-start | bytes 552968 | tf_op jit(solution)/shard_map/ppermute | solution.py:521
  27.2 11.5 %copy-start.15 = (f32[3,3,2,8,128]{4,3,2,1,0:T(8,128)}, f32[3,3,2,8,128]{4,3,2,1,0:T(8,128)S(1)}, u32[]{:S(2)}) copy-start(f32[3,3,2,8,128]{4,3,2,1,0:T(8,128)S(1)} %collective-permute-done.8.refs_18_) | copy-start | bytes 221188
  27.2 1.4 collective-permute-start.6
  27.9 10.8 %copy-start.16 = (f32[3,3,2,8,128]{4,3,2,1,0:T(8,128)}, f32[3,3,2,8,128]{4,3,2,1,0:T(8,128)S(1)}, u32[]{:S(2)}) copy-start(f32[3,3,2,8,128]{4,3,2,1,0:T(8,128)S(1)} %collective-permute-done.7.refs_17_) | copy-start | bytes 221188
  27.9 8.8 %collective-permute-start.5 = (f32[3,3,2,8,128]{4,3,2,1,0:T(8,128)S(1)}, f32[3,3,2,8,128]{4,3,2,1,0:T(8,128)S(1)}, u32[]{:S(2)}, u32[]{:S(2)}) collective-permute-start(f32[3,3,2,8,128]{4,3,2,1,0:T(8,128)S(1)} %get-tuple-element.33), channel_id=1, source_target_pairs={{3,0},{4,7},{11,8},{12,15},{19,16},{20,23},{27,24},{28,31}} | collective-permute-start | bytes 221192 | tf_op jit(solution)/shard_map/ppermute | solution.py:521
  28.5 10.2 %copy-start.17 = (f32[3,3,2,8,128]{4,3,2,1,0:T(8,128)}, f32[3,3,2,8,128]{4,3,2,1,0:T(8,128)S(1)}, u32[]{:S(2)}) copy-start(f32[3,3,2,8,128]{4,3,2,1,0:T(8,128)S(1)} %collective-permute-done.6.refs_16_) | copy-start | bytes 221188
  28.6 10.1 %collective-permute-start.4 = (f32[3,3,2,8,128]{4,3,2,1,0:T(8,128)S(1)}, f32[3,3,2,8,128]{4,3,2,1,0:T(8,128)S(1)}, u32[]{:S(2)}, u32[]{:S(2)}) collective-permute-start(f32[3,3,2,8,128]{4,3,2,1,0:T(8,128)S(1)} %get-tuple-element.34), channel_id=1, source_target_pairs={{2,0},{5,7},{10,8},{13,15},{18,16},{21,23},{26,24},{29,31}} | collective-permute-start | bytes 221192 | tf_op jit(solution)/shard_map/ppermute | solution.py:521
  36.7 2.0 %copy-start.18 = (f32[3,3,2,8,128]{4,3,2,1,0:T(8,128)}, f32[3,3,2,8,128]{4,3,2,1,0:T(8,128)S(1)}, u32[]{:S(2)}) copy-start(f32[3,3,2,8,128]{4,3,2,1,0:T(8,128)S(1)} %collective-permute-done.5.refs_15_) | copy-start | bytes 221188
  36.7 1.9 %collective-permute-start.3 = (f32[3,3,2,8,128]{4,3,2,1,0:T(8,128)S(1)}, f32[3,3,2,8,128]{4,3,2,1,0:T(8,128)S(1)}, u32[]{:S(2)}, u32[]{:S(2)}) collective-permute-start(f32[3,3,2,8,128]{4,3,2,1,0:T(8,128)S(1)} %get-tuple-element.35), channel_id=1, source_target_pairs={{1,0},{6,7},{9,8},{14,15},{17,16},{22,23},{25,24},{30,31}} | collective-permute-start | bytes 221192 | tf_op jit(solution)/shard_map/ppermute | solution.py:521
  53.8 64.5 %collective-permute-start.13 = (f32[3,81,8,128]{3,2,1,0:T(8,128)}, f32[3,81,8,128]{3,2,1,0:T(8,128)S(1)}, u32[]{:S(2)}, u32[]{:S(2)}) collective-permute-start(f32[3,81,8,128]{3,2,1,0:T(8,128)} %get-tuple-element.24), channel_id=1, source_target_pairs={{1,2},{2,1},{3,4},{4,3},{5,6},{6,5},{9,10},{10,9},{11,12},{12,11},... | collective-permute-start | bytes 2985992 | tf_op jit(solution)/shard_map/ppermute | solution.py:495
  56.1 62.3 %collective-permute-start.12 = (f32[3,81,8,128]{3,2,1,0:T(8,128)}, f32[3,81,8,128]{3,2,1,0:T(8,128)S(1)}, u32[]{:S(2)}, u32[]{:S(2)}) collective-permute-start(f32[3,81,8,128]{3,2,1,0:T(8,128)} %get-tuple-element.24), channel_id=1, source_target_pairs={{0,1},{1,0},{2,3},{3,2},{4,5},{5,4},{6,7},{7,6},{8,9},{9,8},{10,11... | collective-permute-start | bytes 2985992 | tf_op jit(solution)/shard_map/ppermute | solution.py:495
  56.2 17.0 %collective-permute-start.19 = (f32[3,17,8,128]{3,2,1,0:T(8,128)}, f32[3,17,8,128]{3,2,1,0:T(8,128)S(1)}, u32[]{:S(2)}, u32[]{:S(2)}) collective-permute-start(f32[3,17,8,128]{3,2,1,0:T(8,128)} %get-tuple-element.25), channel_id=1, source_target_pairs={{9,18},{10,17},{11,20},{12,19},{13,22},{14,21},{17,10},{18,9},{19,... | collective-permute-start | bytes 626696 | tf_op jit(solution)/shard_map/ppermute | solution.py:512
  62.5 17.2 %collective-permute-start.18 = (f32[3,17,8,128]{3,2,1,0:T(8,128)}, f32[3,17,8,128]{3,2,1,0:T(8,128)S(1)}, u32[]{:S(2)}, u32[]{:S(2)}) collective-permute-start(f32[3,17,8,128]{3,2,1,0:T(8,128)} %get-tuple-element.25), channel_id=1, source_target_pairs={{8,17},{9,16},{10,19},{11,18},{12,21},{13,20},{14,23},{15,22},{16,... | collective-permute-start | bytes 626696 | tf_op jit(solution)/shard_map/ppermute | solution.py:512
  64.4 15.3 %collective-permute-start.17 = (f32[3,17,8,128]{3,2,1,0:T(8,128)}, f32[3,17,8,128]{3,2,1,0:T(8,128)S(1)}, u32[]{:S(2)}, u32[]{:S(2)}) collective-permute-start(f32[3,17,8,128]{3,2,1,0:T(8,128)} %get-tuple-element.25), channel_id=1, source_target_pairs={{1,10},{2,9},{3,12},{4,11},{5,14},{6,13},{9,2},{10,1},{11,4},{12,3... | collective-permute-start | bytes 626696 | tf_op jit(solution)/shard_map/ppermute | solution.py:512
  73.1 45.9 %copy-start.4 = (f32[3,17,8,128]{3,2,1,0:T(8,128)}, f32[3,17,8,128]{3,2,1,0:T(8,128)S(1)}, u32[]{:S(2)}) copy-start(f32[3,17,8,128]{3,2,1,0:T(8,128)S(1)} %collective-permute-done.19.refs_14_) | copy-start | bytes 626692
  73.1 10.0 %collective-permute-start.16 = (f32[3,17,8,128]{3,2,1,0:T(8,128)}, f32[3,17,8,128]{3,2,1,0:T(8,128)S(1)}, u32[]{:S(2)}, u32[]{:S(2)}) collective-permute-start(f32[3,17,8,128]{3,2,1,0:T(8,128)} %get-tuple-element.25), channel_id=1, source_target_pairs={{0,9},{1,8},{2,11},{3,10},{4,13},{5,12},{6,15},{7,14},{8,1},{9,0},... | collective-permute-start | bytes 626696 | tf_op jit(solution)/shard_map/ppermute | solution.py:512
  79.7 39.3 %copy-start.5 = (f32[3,17,8,128]{3,2,1,0:T(8,128)}, f32[3,17,8,128]{3,2,1,0:T(8,128)S(1)}, u32[]{:S(2)}) copy-start(f32[3,17,8,128]{3,2,1,0:T(8,128)S(1)} %collective-permute-done.18.refs_13_) | copy-start | bytes 626692
  79.7 38.6 %collective-permute-start.10 = (f32[12,88,128]{2,1,0:T(8,128)}, f32[12,88,128]{2,1,0:T(8,128)S(1)}, u32[]{:S(2)}, u32[]{:S(2)}) collective-permute-start(f32[12,88,128]{2,1,0:T(8,128)} %get-tuple-element.22), channel_id=1, source_target_pairs={{0,8},{8,0},{16,24},{24,16},{1,9},{9,1},{17,25},{25,17},{2,10},{10... | collective-permute-start | bytes 1622024 | tf_op jit(solution)/shard_map/ppermute | solution.py:495
  79.7 39.3 %copy-start.6 = (f32[3,17,8,128]{3,2,1,0:T(8,128)}, f32[3,17,8,128]{3,2,1,0:T(8,128)S(1)}, u32[]{:S(2)}) copy-start(f32[3,17,8,128]{3,2,1,0:T(8,128)S(1)} %collective-permute-done.17.refs_12_) | copy-start | bytes 626692
  79.7 38.6 %collective-permute-start.11 = (f32[12,88,128]{2,1,0:T(8,128)}, f32[12,88,128]{2,1,0:T(8,128)S(1)}, u32[]{:S(2)}, u32[]{:S(2)}) collective-permute-start(f32[12,88,128]{2,1,0:T(8,128)} %get-tuple-element.23), channel_id=1, source_target_pairs={{8,16},{16,8},{9,17},{17,9},{10,18},{18,10},{11,19},{19,11},{12,20... | collective-permute-start | bytes 1622024 | tf_op jit(solution)/shard_map/ppermute | solution.py:495
  83.1 35.9 %copy-start.7 = (f32[3,17,8,128]{3,2,1,0:T(8,128)}, f32[3,17,8,128]{3,2,1,0:T(8,128)S(1)}, u32[]{:S(2)}) copy-start(f32[3,17,8,128]{3,2,1,0:T(8,128)S(1)} %collective-permute-done.16.refs_11_) | copy-start | bytes 626692
  83.1 27.5 %collective-permute-start.15 = (f32[3,17,8,128]{3,2,1,0:T(8,128)}, f32[3,17,8,128]{3,2,1,0:T(8,128)S(1)}, u32[]{:S(2)}, u32[]{:S(2)}) collective-permute-start(f32[3,17,8,128]{3,2,1,0:T(8,128)} %get-tuple-element.25), channel_id=1, source_target_pairs={{8,16},{16,8},{9,17},{17,9},{10,18},{18,10},{11,19},{19,11},{12,20... | collective-permute-start | bytes 626696 | tf_op jit(solution)/shard_map/ppermute | solution.py:495
  110.6 8.4 %copy-start.8 = (f32[3,17,8,128]{3,2,1,0:T(8,128)}, f32[3,17,8,128]{3,2,1,0:T(8,128)S(1)}, u32[]{:S(2)}) copy-start(f32[3,17,8,128]{3,2,1,0:T(8,128)S(1)} %collective-permute-done.15.refs_10_) | copy-start | bytes 626692
  110.6 7.7 %collective-permute-start.14 = (f32[3,17,8,128]{3,2,1,0:T(8,128)}, f32[3,17,8,128]{3,2,1,0:T(8,128)S(1)}, u32[]{:S(2)}, u32[]{:S(2)}) collective-permute-start(f32[3,17,8,128]{3,2,1,0:T(8,128)} %get-tuple-element.25), channel_id=1, source_target_pairs={{0,8},{8,0},{16,24},{24,16},{1,9},{9,1},{17,25},{25,17},{2,10},{10... | collective-permute-start | bytes 626696 | tf_op jit(solution)/shard_map/ppermute | solution.py:495
  118.4 1.4 copy-start
  (9 other events, 7.2 us)
